TPU v7x, 256 devices: a whole 4x4x8 slice. The times are simulated.
256 devices in a mesh: gx: 4 (over y), gy: 8 (over x, core), gz: 8 (over z).
Axes of the slice: x: 4, y: 4, z: 8, core: 2. Of those that a mesh axis runs over, the one named last changes fastest.
Arguments:
- flow_state: float32 [5, 256, 128, 512], P(None, 'gz', 'gy', 'gx'), may hold values from -5 to 120, as said below
- advection: float32 [3, 5], replicated, may hold values from -400 to 400, as said below
- inverse_x: float32 [5, 128, 128], replicated, may hold values from -1 to 1, as said below
- inverse_y: float32 [5, 16, 16], replicated, may hold values from -1 to 1, as said below
- inverse_z: float32 [5, 32, 32], replicated, may hold values from -1 to 1, as said below
- reduced_x: float32 [5, 16, 16], replicated, as said below
- reduced_y: float32 [5, 32, 32], replicated, as said below
- reduced_z: float32 [5, 32, 32], replicated, as said below
Outputs:
- update: float32 [5, 256, 128, 512], P(None, 'gz', 'gy', 'gx')
- rms_norm: float32 [5], replicated
Inputs may be any that keep to these rules, and one draw needn't show every extreme that they name: flow_state[0] (density) lies between 0.5 and 2, and flow_state[4] / density minus half the squared velocity is at least 0.6 in every cell. `advection`: every entry has magnitude between 100 and 400. inverse_x[v] is the inverse of the 128 x 128 matrix with 4 on the diagonal, advection[0, v] / 2 - 2 just above it, -advection[0, v] / 2 - 2 just below it and 0.5 two places off it. inverse_y[v] is the inverse of the 16 x 16 matrix built likewise from advection[1, v]. inverse_z[v] is the inverse of the 32 x 32 matrix built likewise from advection[2, v]. reduced_x[v] is the inverse of I + K, K being the boundary rows and columns of the block inverses times the coupling between blocks, so that S_x equals the exact solution of the banded system along whole x lines with nothing beyond the grid's ends. reduced_y[v] is built likewise for y lines. reduced_z[v] is built likewise for z lines.
All inputs are finite; a program needn't handle non-finite values.
Results may differ from a plain program's by a relative error of at most 0.0002.
Values sent between devices are 32-bit elements.
A program may use at most 64 MiB of HBM per device.

v0:
```python
import jax
import jax.numpy as jnp
import numpy as np
from jax import lax
from jax.sharding import Mesh
from jax.sharding import PartitionSpec as P

GX_GY_GZ = ("gx", "gy_0", "gy_1", "gz")
GY = ("gy_0", "gy_1")


exact_mode = lax.Precision.HIGHEST
gas_ratio = 0.4
courant = 8000.0
damping = 0.0625
fourth_coef = 0.5


def padded_2(shard, sides, width):
    edges = {}
    for axis, dim in sides:
        devices, length = (lax.axis_size(axis), shard.shape[dim])
        up = [(i, (i + 1) % devices) for i in range(devices)]
        last = lax.slice_in_dim(shard, length - width, length, axis=dim)
        first = lax.slice_in_dim(shard, 0, width, axis=dim)
        edges[dim] = (
            lax.ppermute(last, axis, up),
            lax.ppermute(first, axis, [(b, a) for a, b in up]),
        )
    done = []
    for _, dim in sides:
        low, high = edges[dim]
        around = [(width, width) if d in done else (0, 0) for d in range(shard.ndim)]
        shard = jnp.concatenate([jnp.pad(low, around), shard, jnp.pad(high, around)], axis=dim)
        done.append(dim)
    return shard


def collected_together(shard, axis):
    leaves = jax.tree.leaves(shard)
    turns = sorted(range(len(leaves)), key=lambda k: -leaves[k].size)
    width = (1, *leaves[turns[0]].shape)[-1]
    lines = [
        jnp.pad(leaves[k].reshape(-1), (0, -leaves[k].size % width)).reshape(-1, width)
        for k in turns
    ]
    both, at, found = (lax.all_gather(jnp.concatenate(lines), axis), 0, {})
    for k, line in zip(turns, lines):
        section = both[:, at : at + len(line)].reshape(len(both), -1)
        found[k] = section[:, : leaves[k].size].reshape(-1, *leaves[k].shape)
        at += len(line)
    numbers = iter(range(len(leaves)))
    return jax.tree.map(lambda _: found[next(numbers)], shard)


def combined_by_axis(shard, axes, combine):
    for axis in axes:
        pieces = collected_together(shard, axis)
        shard = jax.tree.map(lambda part: part[0], pieces)
        for k in range(1, lax.axis_size(axis)):
            shard = combine(shard, jax.tree.map(lambda part: part[k], pieces))
    return shard


def in_order(parts, dim):
    parts = jnp.moveaxis(parts, 0, dim)
    dims = parts.shape
    return parts.reshape(*dims[:dim], dims[dim] * dims[dim + 1], *dims[dim + 2 :])


def from_everyone(shard, axis):
    devices = lax.axis_size(axis)
    return lax.all_to_all(
        jnp.broadcast_to(shard[None], (devices, *shard.shape)), axis, 0, 0, tiled=True
    )


def gathered_copies(shard, axis, dim):
    return in_order(from_everyone(shard, axis), dim)


def primitives(flow_state):
    density = flow_state[0]
    velocity = flow_state[1:4] / density
    kinetic = 0.5 * jnp.sum(velocity * velocity, axis=0)
    internal = jnp.maximum(flow_state[4] / density - kinetic, 0.25)
    pressure = gas_ratio * density * internal
    return (velocity, internal, pressure)


def fluxes_along(flow_state, direction):
    velocity, internal, pressure = primitives(flow_state)
    carried = velocity[direction]
    columns = [flow_state[1 + direction]]
    for component in range(3):
        moment = flow_state[1 + component] * carried
        if component == direction:
            moment = moment + pressure
        columns.append(moment)
    columns.append((flow_state[4] + pressure) * carried)
    return jnp.stack(columns)


def window(padded, line_axis, offset, margin):
    slices = [slice(None), slice(2, -2), slice(2, -2), slice(2, -2)]
    extent = padded.shape[line_axis] - 4
    slices[line_axis] = slice(2 + offset - margin, 2 + offset + extent + margin)
    return padded[tuple(slices)]


def residual_field(padded):
    centre = window(padded, 1, 0, 0)
    running = jnp.zeros_like(centre)
    for direction in range(3):
        line_axis = 3 - direction
        fluxes = fluxes_along(window(padded, line_axis, 0, 1), direction)
        extent = fluxes.shape[line_axis]
        forward = lax.slice_in_dim(fluxes, 2, extent, axis=line_axis)
        backward = lax.slice_in_dim(fluxes, 0, extent - 2, axis=line_axis)
        running = running - 0.5 * (forward - backward)
        fourth = (
            window(padded, line_axis, -2, 0)
            - 4.0 * window(padded, line_axis, -1, 0)
            + 6.0 * centre
            - 4.0 * window(padded, line_axis, 1, 0)
            + window(padded, line_axis, 2, 0)
        )
        running = running - damping * fourth
    return running


def combine_stats(first, second):
    return (jnp.maximum(first[0], second[0]), first[1] + second[1])


def neighbour_table(reduced):
    blocks = reduced.shape[1] // 4
    padded = jnp.pad(reduced, ((0, 0), (2, 2), (0, 0)))
    picked = (4 * np.arange(blocks)[:, None] + np.array([0, 1, 6, 7])[None, :]).reshape(-1)
    return jnp.transpose(padded[:, picked, :], (1, 0, 2))


def gather_terms(own_rows, carry, piece):
    columns = lax.slice_in_dim(own_rows, 0, piece.shape[1], axis=2)
    return carry + jnp.einsum("rvq,vqn->rvn", columns, piece, precision=exact_mode)


def empty_rows(boundary_rows):
    return jnp.zeros((4, boundary_rows.shape[0], boundary_rows.shape[2]), jnp.float32)


def line_solve(line_field, line_axis, inverse, speeds, nearby):
    block_len = inverse.shape[1]
    patterns = {3: "vij,vzyj->vzyi", 2: "vij,vzjx->vzix", 1: "vij,vjyx->viyx"}
    local_part = jnp.einsum(patterns[line_axis], inverse, line_field, precision=exact_mode)
    boundary = jnp.concatenate(
        [
            lax.slice_in_dim(local_part, 0, 2, axis=line_axis),
            lax.slice_in_dim(local_part, block_len - 2, block_len, axis=line_axis),
        ],
        axis=line_axis,
    )
    boundary_rows = jnp.moveaxis(boundary, line_axis, 1)
    boundary_rows = boundary_rows.reshape(boundary_rows.shape[0], 4, -1)
    nearby_rows = nearby(boundary_rows)
    flat_shape = list(line_field.shape)
    flat_shape[line_axis] = 1
    pieces = [nearby_rows[position].reshape(flat_shape) for position in range(4)]
    factor = speeds.reshape(-1, 1, 1, 1)
    lower_one = -0.5 * factor - 4.0 * fourth_coef
    upper_one = 0.5 * factor - 4.0 * fourth_coef
    left_first = fourth_coef * pieces[0] + lower_one * pieces[1]
    left_second = fourth_coef * pieces[1]
    right_first = fourth_coef * pieces[2]
    right_second = upper_one * pieces[2] + fourth_coef * pieces[3]
    column_shape = [inverse.shape[0], 1, 1, 1]
    column_shape[line_axis] = block_len

    def column(place):
        return inverse[:, :, place].reshape(column_shape)

    correction = (
        column(0) * left_first
        + column(1) * left_second
        + column(block_len - 2) * right_first
        + column(block_len - 1) * right_second
    )
    return local_part - correction


def shards(flow_state, advection, inverse_x, inverse_y, inverse_z, reduced_x, reduced_y, reduced_z):
    velocity, internal, pressure = primitives(flow_state)
    wave_speed = jnp.sum(jnp.abs(velocity), axis=0) + jnp.sqrt(3.0 * 1.4 * gas_ratio * internal)
    local_top = jnp.max(wave_speed)
    padded = padded_2(flow_state, (("gx", 3), (GY, 2), ("gz", 1)), 2)
    residual = residual_field(padded)
    local_sums = jnp.sum(residual * residual, axis=(1, 2, 3))
    top_speed, squares = combined_by_axis((local_top, local_sums), GX_GY_GZ, combine_stats)
    cell_count = (
        residual.shape[1]
        * residual.shape[2]
        * residual.shape[3]
        * lax.axis_size("gx")
        * lax.axis_size(GY)
        * lax.axis_size("gz")
    )
    rms_norm = jnp.sqrt(squares / float(cell_count))
    time_step = courant / top_speed
    table_x = neighbour_table(reduced_x)
    table_y = neighbour_table(reduced_y)
    table_z = neighbour_table(reduced_z)
    index_x = lax.axis_index("gx")
    index_y = lax.axis_index(GY)
    index_z = lax.axis_index("gz")

    def nearby_x(boundary_rows):
        own_rows = lax.dynamic_slice_in_dim(table_x, 4 * index_x, 4, 0)
        return gather_terms(
            own_rows, empty_rows(boundary_rows), gathered_copies(boundary_rows, "gx", 1)
        )

    def nearby_y(boundary_rows):
        own_rows = lax.dynamic_slice_in_dim(table_y, 4 * index_y, 4, 0)
        return gather_terms(
            own_rows, empty_rows(boundary_rows), gathered_copies(boundary_rows, GY, 1)
        )

    def nearby_z(boundary_rows):
        own_rows = lax.dynamic_slice_in_dim(table_z, 4 * index_z, 4, 0)
        return gather_terms(
            own_rows, empty_rows(boundary_rows), gathered_copies(boundary_rows, "gz", 1)
        )

    line_field = residual
    line_field = line_solve(line_field, 3, inverse_x, advection[0], nearby_x)
    line_field = line_solve(line_field, 2, inverse_y, advection[1], nearby_y)
    line_field = line_solve(line_field, 1, inverse_z, advection[2], nearby_z)
    update = time_step * line_field
    return (update, rms_norm)


def solution(mesh):
    torus = Mesh(
        mesh.devices.reshape(mesh.shape["gx"], 4, 2, mesh.shape["gz"]), ("gx", "gy_0", "gy_1", "gz")
    )
    return jax.shard_map(
        shards,
        mesh=torus,
        in_specs=(P(None, "gz", GY, "gx"), P(), P(), P(), P(), P(), P(), P()),
        out_specs=(P(None, "gz", GY, "gx"), P()),
        check_vma=False,
    )
```

profile of v0, /device:TPU:1, one launch (start us, length us, event | category | flops | bytes accessed | tf_op | source)
XLA Modules:
  0.0 195.9 jit_solution(9758615532742740411)
XLA Ops:
  0.6 3.2 %fusion.83 = (f32[5,32,16,2]{3,2,1,0:T(8,128)}, f32[5,32,16,2]{3,2,1,0:T(8,128)S(1)}) fusion(f32[5,32,16,128]{3,2,1,0:T(8,128)} %param.14), kind=kLoop, calls=%fused_computation.221 | loop fusion | bytes 81920 | tf_op jit(solution)/shard_map/slice | solution.py:24
  3.8 2.6 %copy.124 = f32[5,32,16,2]{1,2,3,0:T(8,128)} copy(f32[5,32,16,2]{3,2,1,0:T(8,128)} %get-tuple-element.46) | data formatting | bytes 40960
  6.5 2.1 %collective-permute-start = (f32[5,32,16,2]{1,2,3,0:T(8,128)}, f32[5,32,16,2]{1,2,3,0:T(8,128)}, u32[]{:S(2)}, u32[]{:S(2)}) collective-permute-start(f32[5,32,16,2]{1,2,3,0:T(8,128)} %copy.124), channel_id=1, source_target_pairs={{0,64},{64,128},{128,192},{192,0},{1,65},{65,129},{129,193},{193,1... | collective-permute-start | bytes 61448 | tf_op jit(solution)/shard_map/ppermute | solution.py:27
  8.6 1.2 copy.125
  9.8 1.4 collective-permute-start.1
  11.4 0.7 copy.126
  12.1 2.3 %collective-permute-start.2 = (f32[5,32,2,128]{3,1,2,0:T(8,128)}, f32[5,32,2,128]{3,1,2,0:T(8,128)}, u32[]{:S(2)}, u32[]{:S(2)}) collective-permute-start(f32[5,32,2,128]{3,1,2,0:T(8,128)} %copy.126), channel_id=1, source_target_pairs={{0,8},{8,16},{16,24},{24,32},{32,40},{40,48},{48,56},{56,0},{1,9},... | collective-permute-start | bytes 491528 | tf_op jit(solution)/shard_map/ppermute | solution.py:27
  14.3 0.6 collective-permute-start.3
  15.0 0.6 fusion.81
  15.6 1.0 collective-permute-start.4
  16.7 1.2 fusion.84
  17.9 4.2 %collective-permute-start.5 = (f32[5,2,16,128]{3,2,1,0:T(8,128)S(1)}, f32[5,2,16,128]{3,2,1,0:T(8,128)}, u32[]{:S(2)}, u32[]{:S(2)}) collective-permute-start(f32[5,2,16,128]{3,2,1,0:T(8,128)S(1)} %get-tuple-element.43), channel_id=1, source_target_pairs={{1,0},{2,1},{3,2},{4,3},{5,4},{6,5},{7,6},{0,7},{9,8},{10,9},{11,1... | collective-permute-start | bytes 245768 | tf_op jit(solution)/shard_map/ppermute | solution.py:28
  22.1 1.5 copy.84
  23.6 2.5 %copy.85 = f32[5,32,16,2]{3,2,1,0:T(8,128)} copy(f32[5,32,16,2]{1,2,3,0:T(8,128)} %collective-permute-done.1) | data formatting | bytes 40960 | tf_op jit(solution)/shard_map/ppermute | solution.py:28
  26.1 2.4 %pad_maximum_fusion.1 = f32[5,32,16,132]{3,2,1,0:T(8,128)S(1)} fusion(f32[5,32,16,2]{3,2,1,0:T(8,128)} %copy.85, f32[5,32,16,128]{3,2,1,0:T(8,128)S(1)} %copy-done, f32[5,32,16,2]{3,2,1,0:T(8,128)S(1)} %copy.84), kind=kLoop, calls=%fused_computation.5 | loop fusion | flops 675840 | bytes 2703360 | tf_op jit(solution)/shard_map/concatenate | solution.py:34
  30.7 1.1 pad.40
  31.8 1.0 pad.41
  32.8 1.0 copy.144
  34.3 1.0 copy.145
  36.2 1.9 pad_maximum_fusion
  40.9 9.2 %multiply_reduce_fusion.1 = (f32[5]{0:T(128)S(1)}, f32[5,32,16,128]{3,2,1,0:T(8,128)S(1)}) fusion(f32[5,2,20,132]{3,2,1,0:T(8,128)S(1)} %pad.41, f32[5,32,2,132]{3,2,1,0:T(2,128)S(1)} %pad.39.clone, f32[5,32,16,2]{3,2,1,0:T(8,128)S(1)} %copy-done.1, f32[5,32,16,128]{3,2,1,0:T(8,128)S(1)} %copy-done, f32[5,32,16,2]{3,2,1,0:T(8,128)S(1)} %copy.84, ...), kind=kLoop, calls=%fused_computation.79 | loop fusion | flops 23592956 | bytes 11075860 | tf_op jit(solution)/shard_map/reduce_sum | solution.py:197
  50.1 1.3 fusion.54
  51.4 1.9 fusion.80
  53.3 1.9 copy.96
  55.2 2.5 %copy.97 = f32[5,32,16,2]{1,2,3,0:T(8,128)} copy(f32[5,32,16,2]{3,2,1,0:T(8,128)} %get-tuple-element.41) | data formatting | bytes 40960 | tf_op jit(solution)/shard_map/slice | solution.py:159
  57.8 0.9 maximum_bitcast_fusion.1
  58.7 0.9 copy.98
  59.6 1.2 broadcast_in_dim.34
  60.8 0.7 broadcast_in_dim.35
  61.4 3.3 %all-to-all-start = ((f32[4,5,4,512]{3,2,1,0:T(4,128)}), f32[4,5,4,512]{3,2,1,0:T(4,128)S(1)}, u32[]{:S(2)}, u32[]{:S(2)}) async-start(f32[4,5,4,512]{3,2,1,0:T(4,128)} %broadcast_in_dim.35), calls=%async_computation | async-start | bytes 327680 | tf_op jit(solution)/shard_map/all_to_all | solution.py:73
  64.8 0.7 pad_clamp_fusion
  65.5 0.8 copy.100
  66.3 0.6 pad.46
  66.9 1.2 copy.129
  68.1 1.2 copy.131
  69.6 1.5 gather_fusion
  72.1 3.4 %convolution_bitcast_fusion.3 = f32[5,32,16,128]{3,2,1,0:T(8,128)S(1)} fusion(f32[5,32,16,128]{3,2,1,0:T(8,128)S(1)} %fusion.54, f32[5,32,16]{2,1,0:T(8,128)S(1)} %get-tuple-element.71, f32[5,128]{1,0:T(8,128)S(1)} %bitcast.189, f32[5,32,16]{2,1,0:T(8,128)S(1)} %get-tuple-element.70, f32[5,128]{1,0:T(8,128)S(1)} %bitcast.188, ...), kind=kOutput, calls=%fused_computation.14 | convolution fusion | flops 65536000 | bytes 2677760 | tf_op jit(solution)/shard_map/vij,vzjx->vzix/dot_general | solution.py:155
  75.5 1.0 copy-done.3
  76.8 2.2 %broadcast_in_dim.38 = f32[8,5,4,4096]{3,2,1,0:T(4,128)} broadcast(f32[5,4,4096]{2,1,0:T(4,128)S(1)} %maximum_bitcast_fusion), dimensions={1,2,3} | broadcast | bytes 2949120 | tf_op jit(solution)/shard_map/broadcast_in_dim | solution.py:74
  79.0 6.5 %all-to-all-start.1 = ((f32[8,5,4,4096]{3,2,1,0:T(4,128)}), f32[8,5,4,4096]{3,2,1,0:T(4,128)}, u32[]{:S(2)}, u32[]{:S(2)}) async-start(f32[8,5,4,4096]{3,2,1,0:T(4,128)} %broadcast_in_dim.38), calls=%async_computation.1 | async-start | bytes 5242880 | tf_op jit(solution)/shard_map/all_to_all | solution.py:73
  86.1 0.6 gather_fusion.1
  87.0 0.7 fusion.65
  87.8 29.6 %all-to-all-done.1 = f32[8,5,4,4096]{3,2,1,0:T(4,128)} async-done(((f32[8,5,4,4096]{3,2,1,0:T(4,128)}), f32[8,5,4,4096]{3,2,1,0:T(4,128)}, u32[]{:S(2)}, u32[]{:S(2)}) %all-to-all-start.1) | async-done | bytes 2621472 | tf_op jit(solution)/shard_map/all_to_all | solution.py:73
  117.4 3.6 %copy.106 = f32[5,8,4,4096]{3,2,1,0:T(4,128)} copy(f32[5,8,4,4096]{3,2,0,1:T(4,128)} %bitcast.46) | data formatting | bytes 5242880 | tf_op jit(solution)/shard_map/transpose | solution.py:66
  121.1 4.0 %reshape.550 = f32[5,32,4096]{2,1,0:T(8,128)} reshape(f32[5,8,4,4096]{3,2,1,0:T(4,128)} %copy.106) | data formatting | bytes 5242880 | tf_op jit(solution)/shard_map/reshape | solution.py:68
  125.1 3.2 %convolution_bitcast_fusion = f32[4,5,4096]{2,0,1:T(4,128)S(1)} fusion(f32[5,32,4096]{2,1,0:T(8,128)} %reshape.550, f32[4,5,32]{2,1,0:T(8,128)S(1)} %constant_dynamic-slice_fusion.1), kind=kOutput, calls=%fused_computation.3 | convolution fusion | flops 31457280 | bytes 2951680 | tf_op jit(solution)/shard_map/rvq,vqn->rvn/dot_general | solution.py:145
  128.8 0.8 copy-done.4
  130.1 1.7 convolution_bitcast_fusion.2
  132.0 1.4 broadcast_in_dim.41
  133.3 5.7 %all-to-all-start.2 = ((f32[8,5,4,2048]{3,2,1,0:T(4,128)}), f32[8,5,4,2048]{3,2,1,0:T(4,128)S(1)}, u32[]{:S(2)}, u32[]{:S(2)}) async-start(f32[8,5,4,2048]{3,2,1,0:T(4,128)} %broadcast_in_dim.41), calls=%async_computation.2 | async-start | bytes 2621440 | tf_op jit(solution)/shard_map/all_to_all | solution.py:73
  139.0 0.6 pad_bitcast_fusion.3
  140.7 8.4 %all-gather.4 = f32[4,2,5]{2,1,0:T(2,128)S(1)} all-gather(f32[1,2,5]{2,1,0:T(2,128)S(1)} %maximum_bitcast_fusion.3), channel_id=2, replica_groups=mesh['gx'=4,'gy_0'=4,'gy_1'=2,'gz'=8] {'gx'}, dimensions={0}, use_global_device_ids=true | all-gather | bytes 200 | tf_op jit(solution)/shard_map/all_gather | solution.py:47
  149.2 0.6 fusion.89
  152.4 6.7 %all-gather.5 = f32[4,2,5]{2,1,0:T(2,128)S(1)} all-gather(f32[1,2,5]{2,1,0:T(2,128)S(1)} %maximum_bitcast_fusion.4), channel_id=3, replica_groups=mesh['gx'=4,'gy_0'=4,'gy_1'=2,'gz'=8] {'gy_0'}, dimensions={0}, use_global_device_ids=true | all-gather | bytes 200 | tf_op jit(solution)/shard_map/all_gather | solution.py:47
  159.1 0.6 fusion.88
  162.5 5.9 %all-gather.6 = f32[2,2,5]{2,1,0:T(2,128)S(1)} all-gather(f32[1,2,5]{2,1,0:T(2,128)S(1)} %maximum_bitcast_fusion.5), channel_id=4, replica_groups=mesh['gx'=4,'gy_0'=4,'gy_1'=2,'gz'=8] {'gy_1'}, dimensions={0}, use_global_device_ids=true | all-gather | bytes 120 | tf_op jit(solution)/shard_map/all_gather | solution.py:47
  168.3 0.6 fusion.90
  170.3 12.8 %all-gather.7 = f32[8,2,5]{2,1,0:T(2,128)S(1)} all-gather(f32[1,2,5]{2,1,0:T(2,128)S(1)} %maximum_bitcast_fusion.6), channel_id=5, replica_groups=mesh['gx'=4,'gy_0'=4,'gy_1'=2,'gz'=8] {'gz'}, dimensions={0}, use_global_device_ids=true | all-gather | bytes 360 | tf_op jit(solution)/shard_map/all_gather | solution.py:47
  183.1 0.6 fusion.87
  189.5 1.1 copy.114
  190.7 1.7 reshape.551
  192.4 0.8 convolution_bitcast_fusion.1
  193.5 0.6 subtract_multiply_fusion
  194.1 1.8 copy.120
  (111 shorter events, 12.0 us)
Async XLA Ops:
  3.8 7.4 %copy-start = (f32[5,32,16,128]{3,2,1,0:T(8,128)S(1)}, f32[5,32,16,128]{3,2,1,0:T(8,128)}, u32[]{:S(2)}) copy-start(f32[5,32,16,128]{3,2,1,0:T(8,128)} %param.14) | copy-start | bytes 3932164
  6.5 11.4 %collective-permute-start = (f32[5,32,16,2]{1,2,3,0:T(8,128)}, f32[5,32,16,2]{1,2,3,0:T(8,128)}, u32[]{:S(2)}, u32[]{:S(2)}) collective-permute-start(f32[5,32,16,2]{1,2,3,0:T(8,128)} %copy.124), channel_id=1, source_target_pairs={{0,64},{64,128},{128,192},{192,0},{1,65},{65,129},{129,193},{193,1... | collective-permute-start | bytes 61448 | tf_op jit(solution)/shard_map/ppermute | solution.py:27
  8.6 8.1 %copy-start.2 = (f32[5,128,128]{2,1,0:T(8,128)S(1)}, f32[5,128,128]{2,1,0:T(8,128)}, u32[]{:S(2)}) copy-start(f32[5,128,128]{2,1,0:T(8,128)} %param.16) | copy-start | bytes 983044
  9.8 13.8 %collective-permute-start.1 = (f32[5,32,16,2]{1,2,3,0:T(8,128)}, f32[5,32,16,2]{1,2,3,0:T(8,128)}, u32[]{:S(2)}, u32[]{:S(2)}) collective-permute-start(f32[5,32,16,2]{1,2,3,0:T(8,128)} %copy.125), channel_id=1, source_target_pairs={{64,0},{128,64},{192,128},{0,192},{65,1},{129,65},{193,129},{1,193... | collective-permute-start | bytes 61448 | tf_op jit(solution)/shard_map/ppermute | solution.py:28
  12.1 20.8 %collective-permute-start.2 = (f32[5,32,2,128]{3,1,2,0:T(8,128)}, f32[5,32,2,128]{3,1,2,0:T(8,128)}, u32[]{:S(2)}, u32[]{:S(2)}) collective-permute-start(f32[5,32,2,128]{3,1,2,0:T(8,128)} %copy.126), channel_id=1, source_target_pairs={{0,8},{8,16},{16,24},{24,32},{32,40},{40,48},{48,56},{56,0},{1,9},... | collective-permute-start | bytes 491528 | tf_op jit(solution)/shard_map/ppermute | solution.py:27
  14.3 19.9 %collective-permute-start.3 = (f32[5,32,2,128]{3,1,2,0:T(8,128)S(1)}, f32[5,32,2,128]{3,1,2,0:T(8,128)}, u32[]{:S(2)}, u32[]{:S(2)}) collective-permute-start(f32[5,32,2,128]{3,1,2,0:T(8,128)S(1)} %copy.127), channel_id=1, source_target_pairs={{8,0},{16,8},{24,16},{32,24},{40,32},{48,40},{56,48},{0,56},{9,1},... | collective-permute-start | bytes 491528 | tf_op jit(solution)/shard_map/ppermute | solution.py:28
  15.6 2.3 %copy-start.10 = (f32[3,5]{1,0:T(4,128)S(1)}, f32[3,5]{1,0:T(4,128)}, u32[]{:S(2)}) copy-start(f32[3,5]{1,0:T(4,128)} %param.15) | copy-start | bytes 184
  15.6 15.0 %collective-permute-start.4 = (f32[5,2,16,128]{3,2,1,0:T(8,128)}, f32[5,2,16,128]{3,2,1,0:T(8,128)}, u32[]{:S(2)}, u32[]{:S(2)}) collective-permute-start(f32[5,2,16,128]{3,2,1,0:T(8,128)} %get-tuple-element.42), channel_id=1, source_target_pairs={{0,1},{1,2},{2,3},{3,4},{4,5},{5,6},{6,7},{7,0},{8,9},{9,10},{10,1... | collective-permute-start | bytes 245768 | tf_op jit(solution)/shard_map/ppermute | solution.py:27
  17.9 13.9 %collective-permute-start.5 = (f32[5,2,16,128]{3,2,1,0:T(8,128)S(1)}, f32[5,2,16,128]{3,2,1,0:T(8,128)}, u32[]{:S(2)}, u32[]{:S(2)}) collective-permute-start(f32[5,2,16,128]{3,2,1,0:T(8,128)S(1)} %get-tuple-element.43), channel_id=1, source_target_pairs={{1,0},{2,1},{3,2},{4,3},{5,4},{6,5},{7,6},{0,7},{9,8},{10,9},{11,1... | collective-permute-start | bytes 245768 | tf_op jit(solution)/shard_map/ppermute | solution.py:28
  30.6 5.1 %copy-start.1 = (f32[5,32,16,2]{3,2,1,0:T(8,128)S(1)}, f32[5,32,16,2]{3,2,1,0:T(8,128)}, u32[]{:S(2)}) copy-start(f32[5,32,16,2]{3,2,1,0:T(8,128)} %copy.85) | copy-start | bytes 61444
  55.2 9.6 %copy-start.11 = (s32[16]{0:T(128)S(1)}, s32[16]{0:T(128)}, u32[]{:S(2)}) copy-start(s32[16]{0:T(128)} %constant.116) | copy-start | bytes 196
  57.8 11.5 %copy-start.6 = (f32[5,128,1]{2,1,0:T(8,128)S(1)}, f32[5,128,1]{2,1,0:T(8,128)}, u32[]{:S(2)}) copy-start(f32[5,128,1]{2,1,0:T(8,128)} %get-tuple-element.53) | copy-start | bytes 7684
  61.4 9.7 %all-to-all-start = ((f32[4,5,4,512]{3,2,1,0:T(4,128)}), f32[4,5,4,512]{3,2,1,0:T(4,128)S(1)}, u32[]{:S(2)}, u32[]{:S(2)}) async-start(f32[4,5,4,512]{3,2,1,0:T(4,128)} %broadcast_in_dim.35), calls=%async_computation | async-start | bytes 327680 | tf_op jit(solution)/shard_map/all_to_all | solution.py:73
  69.4 2.6 %copy-start.7 = (f32[5,16,16]{2,1,0:T(8,128)S(1)}, f32[5,16,16]{2,1,0:T(8,128)}, u32[]{:S(2)}) copy-start(f32[5,16,16]{2,1,0:T(8,128)} %param.17) | copy-start | bytes 15364
  75.5 1.1 copy-start.3
  79.0 6.5 %copy-start.8 = (f32[5,32,32]{2,1,0:T(8,128)S(1)}, f32[5,32,32]{2,1,0:T(8,128)}, u32[]{:S(2)}) copy-start(f32[5,32,32]{2,1,0:T(8,128)} %param.20) | copy-start | bytes 61444
  79.0 38.5 %all-to-all-start.1 = ((f32[8,5,4,4096]{3,2,1,0:T(4,128)}), f32[8,5,4,4096]{3,2,1,0:T(4,128)}, u32[]{:S(2)}, u32[]{:S(2)}) async-start(f32[8,5,4,4096]{3,2,1,0:T(4,128)} %broadcast_in_dim.38), calls=%async_computation.1 | async-start | bytes 5242880 | tf_op jit(solution)/shard_map/all_to_all | solution.py:73
  86.8 0.9 copy-start.5
  128.3 1.3 copy-start.4
  133.3 6.4 %copy-start.9 = (f32[5,32,32]{2,1,0:T(8,128)S(1)}, f32[5,32,32]{2,1,0:T(8,128)}, u32[]{:S(2)}) copy-start(f32[5,32,32]{2,1,0:T(8,128)} %param.21) | copy-start | bytes 61444
  133.3 56.2 %all-to-all-start.2 = ((f32[8,5,4,2048]{3,2,1,0:T(4,128)}), f32[8,5,4,2048]{3,2,1,0:T(4,128)S(1)}, u32[]{:S(2)}, u32[]{:S(2)}) async-start(f32[8,5,4,2048]{3,2,1,0:T(4,128)} %broadcast_in_dim.41), calls=%async_computation.2 | async-start | bytes 2621440 | tf_op jit(solution)/shard_map/all_to_all | solution.py:73
where the time goes:
time: 199 us; the launch traced here: 196 us
  local copies, waits for them, and re-layouts  57.7 us (29%)
  blocking collectives  33.8 us (17%)
  waiting for transfers between devices  29.6 us (15%)
  starting transfers between devices  27.3 us (14%)
  other arithmetic  24 us (12%)
  between operations  13 us (7%)
  matrix products  10.5 us (5%)
    all_gather x4, blocking collectives, collected_together(): both, at, found = (lax.all_gather(jnp.concatenate(lines), axis), 0, {})  33.8 us
    all_to_all x3, waiting for transfers between devices, from_everyone(): lax.all_to_all(jnp.broadcast_to(shard[None], (devices, *shard.shape)), ax...  29.6 us
    all_to_all x3, starting transfers between devices, from_everyone(): lax.all_to_all(jnp.broadcast_to(shard[None], (devices, *shard.shape)), ax...  15.6 us
    unnamed x46, local copies, waits for them, and re-layouts  14.9 us
    reduce_sum x1, other arithmetic, shards(): local_sums = jnp.sum(residual * residual, axis=(1, 2, 3))  9.21 us
    dot_general x3, matrix products, line_solve(): jnp.einsum(patterns[line_axis], inverse, line_field, precision=exact_mode)  6.31 us
    ppermute x3, starting transfers between devices, padded_2(): lax.ppermute(first, axis, [(b, a) for a, b in up])  6.26 us
    reshape x3, local copies, waits for them, and re-layouts, in_order(): parts.reshape(*dims[:dim], dims[dim] * dims[dim + 1], *dims[dim + 2:])  5.79 us
  transfers between devices with their start and end apart: 9, of which 1 were waited for; matrix products, arithmetic and copies ran while one was open for 15% of the time, Pallas kernels for 0%

commit v1 on v0

v1 whole, which is shorter than its diff:
```python
import functools

import jax
import jax.numpy as jnp
from jax import lax
from jax.experimental import pallas as pl
from jax.experimental.pallas import tpu as pltpu
from jax.sharding import PartitionSpec as P

VARS, CX, CY, CZ = 5, 128, 16, 32
PLANE = CY
ROWS = CZ * CY
F32, BF16 = jnp.float32, jnp.bfloat16
MESH = pl.DeviceIdType.MESH
NT = (((1,), (1,)), ((), ()))


def iota(shape, dim):
    return lax.broadcasted_iota(jnp.int32, shape, dim)


def log2(n):
    return n.bit_length() - 1


def split(x):
    hi = x.astype(BF16)
    return hi, (x - hi.astype(F32)).astype(BF16)


def dot(a, b):
    return jnp.dot(a, b, preferred_element_type=F32)


def dot_nt(a, b):
    return lax.dot_general(a, b, NT, preferred_element_type=F32)


def mm3(left_hi, left_lo, right):
    hi, lo = split(right)
    return dot(left_hi, hi) + (dot(left_hi, lo) + dot(left_lo, hi))


def nt3(a_hi, a_lo, b_hi, b_lo):
    return dot_nt(a_hi, b_hi) + (dot_nt(a_lo, b_hi) + dot_nt(a_hi, b_lo))


def one_hot(cond):
    return jnp.where(cond, 1.0, 0.0).astype(BF16)


def edge(k, length):
    return jnp.where(k < 2, k, k + (length - 4))


def expand(parts, rows, row_map, cols, col_map):
    n, m = parts[0].shape
    row_i, _ = row_map(iota((rows, n), 0))
    pick_rows = one_hot(row_i == iota((rows, n), 1))
    col_j, _ = col_map(iota((m, cols), 1))
    pick_cols = one_hot(col_j == iota((m, cols), 0))
    _, row_r = row_map(iota((rows, cols), 0))
    _, col_c = col_map(iota((rows, cols), 1))
    keep = row_r == col_c
    return [
        jnp.where(keep, dot(pick_rows, dot(part, pick_cols).astype(BF16)), 0.0).astype(BF16)
        for part in parts
    ]


def coupling(shape, blocks_row, speed, row_of):
    row, col = iota(shape, 0), iota(shape, 1)
    base, k = row_of(row)
    lower, upper = -0.5 * speed - 2.0, 0.5 * speed - 2.0
    out = jnp.where((k == 0) & (col == base - 2), 0.5, 0.0)
    out = out + jnp.where((k == 0) & (col == base - 1), lower, 0.0)
    out = out + jnp.where((k == 1) & (col == base - 1), 0.5, 0.0)
    out = out + jnp.where((k == 2) & (col == base + 4), 0.5, 0.0)
    out = out + jnp.where((k == 3) & (col == base + 4), upper, 0.0)
    return out + jnp.where((k == 3) & (col == base + 5), 0.5, 0.0)


def primitives(u):
    scale = 1.0 / u[0]
    vel = [u[1] * scale, u[2] * scale, u[3] * scale]
    kinetic = 0.5 * (vel[0] * vel[0] + vel[1] * vel[1] + vel[2] * vel[2])
    internal = jnp.maximum(u[4] * scale - kinetic, 0.25)
    return vel, internal, 0.4 * u[0] * internal


def fluxes(u, w, pressure, direction):
    out = [u[1 + direction]]
    for c in range(3):
        moment = u[1 + c] * w
        out.append(moment + pressure if c == direction else moment)
    return out + [(u[4] + pressure) * w]


def kernel(
    px, py, pz,
    adv, flow, inv_x, inv_y, inv_z, red_x, red_y, red_z,
    out, rms,
    U, PR, YS, YH, FYH, PK, XH, XC, F, XL, YL, ZL, XR, CT,
    YF, YR1, Y2, YR2, ZF, ZR1, Z2, ZR2, STX, STY, STZ,
    AX, WX, LX, PY, PZ, KY, KZ, WY, WZ,
    in_sem, out_sem, hs, hr, xs, xrv, ysem, yr1s, y2sem, yr2s, zsem, zr1s, z2sem, zr2s, ss, sr,
):
    ix, iy, iz = lax.axis_index("gx"), lax.axis_index("gy"), lax.axis_index("gz")
    zc, yc = CZ // py, CY // pz
    yr, zr = 4 * zc, 4 * yc
    lzc, lyc, lyr, lzr = log2(zc), log2(yc), log2(4 * zc), log2(4 * yc)

    def peer(axis, d):
        me, n = {"gx": (ix, px), "gy": (iy, py), "gz": (iz, pz)}[axis]
        return {axis: (me + d + n) & (n - 1)}

    def remote(src, dst, send, recv, device):
        return pltpu.make_async_remote_copy(
            src_ref=src, dst_ref=dst, send_sem=send, recv_sem=recv,
            device_id=device, device_id_type=MESH,
        )

    def drain(ref, sem):
        pltpu.make_async_copy(ref, ref, sem).wait()

    load = pltpu.make_async_copy(flow, U.at[:, pl.ds(2 * PLANE, ROWS)], in_sem)
    load.start()
    barrier = pltpu.get_barrier_semaphore()
    for axis, n in (("gz", pz), ("gy", py), ("gx", px)):
        for d in range(1, n):
            pl.semaphore_signal(barrier, inc=1, device_id=peer(axis, d), device_id_type=MESH)
    load.wait()

    def pack_rows(v, carry):
        for r in range(2):
            for t in range(CZ // 8):
                for side, first in ((0, CY - 2), (1, 0)):
                    start = 2 * PLANE + 8 * t * PLANE + first + r
                    YS[side, v, pl.ds(r * CZ + 8 * t, 8), :] = U[v, pl.ds(start, 8, stride=PLANE), :]
        return carry

    lax.fori_loop(0, VARS, pack_rows, 0)
    lane = iota((CY, CX), 1)
    row = iota((CY, CX), 0)

    def pack_lanes(z, acc):
        base = pl.multiple_of(2 * PLANE + z * PLANE, PLANE)
        here = (lane >> 2) == z
        return [
            jnp.where(here, pltpu.roll(U[v, pl.ds(base, PLANE), :], 4 * z + 2, 1), acc[v])
            for v in range(VARS)
        ]

    packed = lax.fori_loop(0, CZ, pack_lanes, [jnp.zeros((CY, CX), F32)] * VARS)
    for v in range(VARS):
        PK[v] = packed[v]

    pl.semaphore_wait(barrier, px + py + pz - 3)
    last = 2 * PLANE + ROWS
    halos = [
        remote(flow.at[:, pl.ds(ROWS - 2 * PLANE, 2 * PLANE)], U.at[:, pl.ds(0, 2 * PLANE)],
               hs.at[0], hr.at[0], peer("gz", 1)),
        remote(flow.at[:, pl.ds(0, 2 * PLANE)], U.at[:, pl.ds(last, 2 * PLANE)],
               hs.at[1], hr.at[1], peer("gz", -1)),
        remote(YS.at[0], YH.at[0], hs.at[2], hr.at[2], peer("gy", 1)),
        remote(YS.at[1], YH.at[1], hs.at[3], hr.at[3], peer("gy", -1)),
        remote(PK, XH.at[0], hs.at[4], hr.at[4], peer("gx", 1)),
        remote(PK, XH.at[1], hs.at[5], hr.at[5], peer("gx", -1)),
    ]
    for copy in halos:
        copy.start()

    def plane_primitives(base):
        u = [U[v, pl.ds(base, PLANE), :] for v in range(VARS)]
        vel, internal, pressure = primitives(u)
        for c in range(3):
            PR[c, pl.ds(base, PLANE), :] = vel[c]
        PR[3, pl.ds(base, PLANE), :] = pressure
        return vel, internal

    def first_pass(z, top):
        base = pl.multiple_of(2 * PLANE + z * PLANE, PLANE)
        vel, internal = plane_primitives(base)
        speed = jnp.abs(vel[0]) + jnp.abs(vel[1]) + jnp.abs(vel[2]) + jnp.sqrt(3.0 * 1.4 * 0.4 * internal)
        return jnp.maximum(top, speed)

    top = lax.fori_loop(0, CZ, first_pass, jnp.zeros((CY, CX), F32))

    def build_first(v, carry):
        x_hi, x_lo = split(inv_x[v])
        AX[0, v], AX[1, v] = x_hi, x_lo
        col = iota((CX, CX), 1)
        pick = one_hot(((col >> 2) == v) & (iota((CX, CX), 0) == edge(col & 3, CX)))
        WX[0, v], WX[1, v] = dot(x_hi, pick).astype(BF16), dot(x_lo, pick).astype(BF16)

        def y_row(r):
            s = r - 256
            face = (edge((s >> lzc) & 3, CY), ((s >> lyr) << lzc) + (s & (zc - 1)))
            return jnp.where(s < 0, r >> 4, face[0]), jnp.where(s < 0, r & 15, face[1])

        PY[0, v], PY[1, v] = expand(split(inv_y[v]), 320, y_row, 256, lambda c: (c & 15, c >> 4))
        return carry

    lax.fori_loop(0, VARS, build_first, 0)
    for t in range(3):
        acc = jnp.zeros((8, 8 * px), F32)
        for v in (2 * t, 2 * t + 1):
            if v == VARS:
                continue
            shape = (8, 4 * px)
            own = coupling(shape, 8, adv[0, v], lambda r: (4 * ix, r & 3))
            rows = jnp.dot(own, red_x[v], precision=lax.Precision.HIGHEST, preferred_element_type=F32)
            r, c = iota((4 * px, 8 * px), 0), iota((4 * px, 8 * px), 1)
            spread = jnp.where(r == ((c >> 3) << 2) + (c & 3), 1.0, 0.0)
            wide = jnp.dot(rows, spread, precision=lax.Precision.HIGHEST, preferred_element_type=F32)
            r, c = iota((8, 8 * px), 0), iota((8, 8 * px), 1)
            acc = acc + jnp.where(((r >> 2) == v - 2 * t) & (((c >> 2) & 1) == v - 2 * t), wide, 0.0)
        LX[t] = acc

    for copy in halos:
        copy.wait_recv()
    plane_primitives(PLANE)
    plane_primitives(last)
    for side in range(2):
        mine = pl.ds((1 - side) * CZ, CZ)
        u = [YH[side, v, mine, :] for v in range(VARS)]
        vel, _, pressure = primitives(u)
        for v, f in enumerate(fluxes(u, vel[1], pressure, 1)):
            FYH[side, v] = f
    j = lane & 3
    near = [jnp.where(j < 2, XH[0, v], XH[1, v]) for v in range(VARS)]
    mine = [PK[v] for v in range(VARS)]
    vel, _, pressure = primitives(near)
    near_flux = fluxes(near, vel[0], pressure, 0)
    vel, _, pressure = primitives(mine)
    mine_flux = fluxes(mine, vel[0], pressure, 0)
    for v in range(VARS):
        du, df = near[v] - mine[v], near_flux[v] - mine_flux[v]
        far = -0.0625 * jnp.where(j < 2, pltpu.roll(du, CX - 2, 1), pltpu.roll(du, 2, 1))
        right = pltpu.roll(-0.5 * df + 0.25 * du, CX - 1, 1)
        left = pltpu.roll(0.5 * df + 0.25 * du, 1, 1)
        XC[v] = far + jnp.where(j == 1, right, 0.0) + jnp.where(j == 2, left, 0.0)

    ends = ((lane + 2) & (CX - 1)) < 4

    def second_pass(z, sums):
        base = pl.multiple_of(2 * PLANE + z * PLANE, PLANE)

        def at(ref, k, step):
            return ref[k, pl.ds(base + step * PLANE, PLANE), :]

        u = [at(U, v, 0) for v in range(VARS)]
        ahead = [at(U, v, 1) for v in range(VARS)]
        behind = [at(U, v, -1) for v in range(VARS)]
        pressure = at(PR, 3, 0)
        x_flux = fluxes(u, at(PR, 0, 0), pressure, 0)
        y_flux = fluxes(u, at(PR, 1, 0), pressure, 1)
        z_ahead = fluxes(ahead, at(PR, 2, 1), at(PR, 3, 1), 2)
        z_behind = fluxes(behind, at(PR, 2, -1), at(PR, 3, -1), 2)
        done = []
        for v in range(VARS):
            f = u[v]

            def halo(ref, side, line):
                return jnp.broadcast_to(ref[side, v, pl.ds(line + z, 1), :], (CY, CX))

            low2, low1 = halo(YH, 0, 0), halo(YH, 0, CZ)
            high1, high2 = halo(YH, 1, 0), halo(YH, 1, CZ)
            y_m1 = jnp.where(row == 0, low1, pltpu.roll(f, 1, 0))
            y_m2 = jnp.where(row == 0, low2, jnp.where(row == 1, low1, pltpu.roll(f, 2, 0)))
            y_p1 = jnp.where(row == CY - 1, high1, pltpu.roll(f, CY - 1, 0))
            y_p2 = jnp.where(row == CY - 1, high2, jnp.where(row == CY - 2, high1, pltpu.roll(f, CY - 2, 0)))
            y_fwd = jnp.where(row == CY - 1, halo(FYH, 1, 0), pltpu.roll(y_flux[v], CY - 1, 0))
            y_back = jnp.where(row == 0, halo(FYH, 0, 0), pltpu.roll(y_flux[v], 1, 0))
            near1 = (ahead[v] + behind[v]) + (y_m1 + y_p1) + (pltpu.roll(f, 1, 1) + pltpu.roll(f, CX - 1, 1))
            near2 = (at(U, v, 2) + at(U, v, -2)) + (y_m2 + y_p2) + (pltpu.roll(f, 2, 1) + pltpu.roll(f, CX - 2, 1))
            slope = (z_ahead[v] - z_behind[v]) + (y_fwd - y_back)
            slope = slope + (pltpu.roll(x_flux[v], CX - 1, 1) - pltpu.roll(x_flux[v], 1, 1))
            fix = jnp.where(ends, pltpu.roll(XC[v], (2 * CX - 2 - 4 * z) & (CX - 1), 1), 0.0)
            r = fix - 0.5 * slope - 0.0625 * near2 + 0.25 * near1 - 1.125 * f
            F[v, pl.ds(pl.multiple_of(z * PLANE, PLANE), PLANE), :] = r
            done.append(sums[v] + r * r)
        return done

    sums = lax.fori_loop(0, CZ, second_pass, [jnp.zeros((CY, CX), F32)] * VARS)

    row8 = iota((8, 4 * CX), 0)
    for t in range(3):
        pair = []
        for v in (2 * t, 2 * t + 1):
            if v == VARS:
                pair.append(jnp.zeros((8, ROWS), F32))
                continue
            tile = jnp.where(iota((8, CX), 0) < 2, inv_x[v, 0:8, :], pltpu.roll(inv_x[v, CX - 8 : CX, :], 4, 0))
            if v & 1:
                tile = pltpu.roll(tile, 4, 0)
            pair.append(nt3(*split(tile), *split(F[v])))
        XR[t, ix] = jnp.where(row8 < 4, pair[0], pair[1])
    for d in range(1, px):
        remote(XR.at[:, ix], XR.at[:, ix], xs, xrv, peer("gx", d)).start()

    stat_row = iota((8, CX), 0)
    tile = jnp.where(stat_row == VARS, jnp.max(top), 0.0)
    for v in range(VARS):
        tile = jnp.where(stat_row == v, jnp.sum(sums[v]), tile)
    STX[ix] = tile
    for d in range(1, px):
        remote(STX.at[ix], STX.at[ix], ss.at[0], sr.at[0], peer("gx", d)).start()

    def combine(ref, n):
        total = ref[0]
        for k in range(1, n):
            total = jnp.where(stat_row == VARS, jnp.maximum(total, ref[k]), total + ref[k])
        return total

    def local_x(v, carry):
        XL[v] = nt3(*split(F[v]), AX[0, v], AX[1, v])

        def z_row(r):
            s = r - 256
            face = (edge((s >> lyc) & 3, CZ), ((s >> lzr) << lyc) + (s & (yc - 1)))
            return jnp.where(s < 0, r >> 3, face[0]), jnp.where(s < 0, r & 7, face[1])

        PZ[0, v], PZ[1, v] = expand(split(inv_z[v]), 288, z_row, 256, lambda c: (c & 31, c >> 5))

        def reduced(red, n, speed):
            g = coupling((4 * n, 4 * n), n, speed, lambda r: ((r >> 2) << 2, r & 3))
            return split(jnp.dot(g, red, precision=lax.Precision.HIGHEST, preferred_element_type=F32))

        y_side = lambda r: (r >> lzc, r & (zc - 1))
        KY[0, v], KY[1, v] = expand(reduced(red_y[v], py, adv[1, v]), 4 * CZ, y_side, 4 * CZ, y_side)
        z_side = lambda r: (r >> lyc, r & (yc - 1))
        KZ[0, v], KZ[1, v] = expand(reduced(red_z[v], pz, adv[2, v]), 4 * CY, z_side, 4 * CY, z_side)
        return carry

    lax.fori_loop(0, VARS, local_x, 0)

    drain(XR.at[:, pl.ds(0, px - 1)], xrv)
    factors = [mm3(*split(LX[t]), XR[t].reshape(8 * px, ROWS)) for t in range(3)]
    factors = jnp.concatenate(factors + [jnp.zeros((CX - 24, ROWS), F32)], axis=0).T
    CT[0], CT[1] = split(factors)

    def send_y(src, dst, v, send, recv):
        for d in range(1, py):
            to = peer("gy", d)
            remote(src.at[v, pl.ds(pl.multiple_of(to["gy"] * yr, yr), yr)],
                   dst.at[v, pl.ds(pl.multiple_of(iy * yr, yr), yr)], send, recv, to).start()
        mine = pl.ds(pl.multiple_of(iy * yr, yr), yr)
        dst[v, mine, :] = src[v, mine, :]

    def send_z(src, dst, v, send, recv):
        for d in range(1, pz):
            to = peer("gz", d)
            remote(src.at[v, pl.ds(pl.multiple_of(to["gz"] * zr, zr), zr)],
                   dst.at[v, pl.ds(pl.multiple_of(iz * zr, zr), zr)], send, recv, to).start()
        mine = pl.ds(pl.multiple_of(iz * zr, zr), zr)
        dst[v, mine, :] = src[v, mine, :]

    def local_y(v, carry):
        field = XL[v] - nt3(CT[0], CT[1], WX[0, v], WX[1, v])
        for g in range(2):
            solved = mm3(PY[0, v], PY[1, v], field[256 * g : 256 * g + 256])
            for y in range(CY):
                YL[v, pl.ds(y * CZ + 16 * g, 16), :] = solved[16 * y : 16 * y + 16]
            YF[v, pl.ds(64 * g, 64), :] = solved[256:320]
        send_y(YF, YR1, v, ysem, yr1s.at[v])
        return carry

    lax.fori_loop(0, VARS, local_y, 0)
    drain(STX.at[pl.ds(0, px - 1)], sr.at[0])
    STY[iy] = combine(STX, px)
    for d in range(1, py):
        remote(STY.at[iy], STY.at[iy], ss.at[1], sr.at[1], peer("gy", d)).start()

    def build_last(v, carry):
        WY[0, v], WY[1, v] = expand(
            split(inv_y[v]), ROWS, lambda r: (r >> 5, r & 31),
            4 * CZ, lambda c: (edge((c >> lzc) & 3, CY), ((c >> lyr) << lzc) + (c & (zc - 1))),
        )
        WZ[0, v], WZ[1, v] = expand(
            split(inv_z[v]), ROWS, lambda r: (r >> 4, r & 15),
            4 * CY, lambda c: (edge((c >> lyc) & 3, CZ), ((c >> lzr) << lyc) + (c & (yc - 1))),
        )
        return carry

    lax.fori_loop(0, VARS, build_last, 0)

    def reduced_y(v, carry):
        drain(YR1.at[v, pl.ds(0, (py - 1) * yr)], yr1s.at[v])
        Y2[v] = mm3(KY[0, v], KY[1, v], YR1[v])
        send_y(Y2, YR2, v, y2sem, yr2s.at[v])
        return carry

    lax.fori_loop(0, VARS, reduced_y, 0)
    drain(STY.at[pl.ds(0, py - 1)], sr.at[1])
    STZ[iz] = combine(STY, py)
    for d in range(1, pz):
        remote(STZ.at[iz], STZ.at[iz], ss.at[2], sr.at[2], peer("gz", d)).start()

    def local_z(v, carry):
        drain(YR2.at[v, pl.ds(0, (py - 1) * yr)], yr2s.at[v])
        field = YL[v] - mm3(WY[0, v], WY[1, v], YR2[v])
        for g in range(2):
            solved = mm3(PZ[0, v], PZ[1, v], field[256 * g : 256 * g + 256])
            for z in range(CZ):
                ZL[v, pl.ds(z * CY + 8 * g, 8), :] = solved[8 * z : 8 * z + 8]
            ZF[v, pl.ds(32 * g, 32), :] = solved[256:288]
        send_z(ZF, ZR1, v, zsem, zr1s.at[v])
        return carry

    lax.fori_loop(0, VARS, local_z, 0)

    def reduced_z(v, carry):
        drain(ZR1.at[v, pl.ds(0, (pz - 1) * zr)], zr1s.at[v])
        Z2[v] = mm3(KZ[0, v], KZ[1, v], ZR1[v])
        send_z(Z2, ZR2, v, z2sem, zr2s.at[v])
        return carry

    lax.fori_loop(0, VARS, reduced_z, 0)
    drain(STZ.at[pl.ds(0, pz - 1)], sr.at[2])
    stats = combine(STZ, pz)
    step = 8000.0 / stats[VARS : VARS + 1]
    norms = jnp.sqrt(stats / float(px * py * pz * ROWS * CX))
    for v in range(VARS):
        rms[v] = jnp.max(norms[v : v + 1])

    def finish(v, carry):
        drain(ZR2.at[v, pl.ds(0, (pz - 1) * zr)], zr2s.at[v])
        F[v] = step * (ZL[v] - mm3(WZ[0, v], WZ[1, v], ZR2[v]))
        pltpu.make_async_copy(F.at[v], out.at[v], out_sem).start()
        return carry

    lax.fori_loop(0, VARS, finish, 0)
    for copy in halos:
        copy.wait_send()
    drain(XR.at[:, pl.ds(0, px - 1)], xs)
    drain(STX.at[pl.ds(0, px - 1)], ss.at[0])
    drain(STY.at[pl.ds(0, py - 1)], ss.at[1])
    drain(STZ.at[pl.ds(0, pz - 1)], ss.at[2])
    drain(YF.at[:, pl.ds(0, (py - 1) * yr)], ysem)
    drain(Y2.at[:, pl.ds(0, (py - 1) * yr)], y2sem)
    drain(ZF.at[:, pl.ds(0, (pz - 1) * zr)], zsem)
    drain(Z2.at[:, pl.ds(0, (pz - 1) * zr)], z2sem)
    drain(F, out_sem)


def shards(px, py, pz, flow_state, advection, *tables):
    vmem = pl.BlockSpec(memory_space=pltpu.VMEM)
    smem = pl.BlockSpec(memory_space=pltpu.SMEM)
    hbm = pl.BlockSpec(memory_space=pl.ANY)
    f32 = lambda *shape: pltpu.VMEM(shape, F32)
    b16 = lambda *shape: pltpu.VMEM(shape, BF16)
    dma = pltpu.SemaphoreType.DMA
    field = (VARS, ROWS, CX)
    padded_rows = ROWS + 4 * PLANE
    update, rms = pl.pallas_call(
        functools.partial(kernel, px, py, pz),
        out_shape=(jax.ShapeDtypeStruct(field, F32), jax.ShapeDtypeStruct((VARS,), F32)),
        in_specs=[smem, hbm] + [vmem] * 6,
        out_specs=(hbm, smem),
        scratch_shapes=[
            f32(VARS, padded_rows, CX), f32(4, padded_rows, CX),
            f32(2, VARS, 2 * CZ, CX), f32(2, VARS, 2 * CZ, CX), f32(2, VARS, CZ, CX),
            f32(VARS, CY, CX), f32(2, VARS, CY, CX), f32(VARS, CY, CX),
            f32(*field), f32(*field), f32(*field), f32(*field),
            f32(3, px, 8, ROWS), b16(2, ROWS, CX),
            f32(VARS, 4 * CZ, CX), f32(VARS, 4 * CZ, CX), f32(VARS, 4 * CZ, CX), f32(VARS, 4 * CZ, CX),
            f32(VARS, 4 * CY, CX), f32(VARS, 4 * CY, CX), f32(VARS, 4 * CY, CX), f32(VARS, 4 * CY, CX),
            f32(px, 8, CX), f32(py, 8, CX), f32(pz, 8, CX),
            b16(2, VARS, CX, CX), b16(2, VARS, CX, CX), f32(3, 8, 8 * px),
            b16(2, VARS, 320, 256), b16(2, VARS, 288, 256),
            b16(2, VARS, 4 * CZ, 4 * CZ), b16(2, VARS, 4 * CY, 4 * CY),
            b16(2, VARS, ROWS, 4 * CZ), b16(2, VARS, ROWS, 4 * CY),
            dma, dma, dma((6,)), dma((6,)), dma, dma,
            dma, dma((VARS,)), dma, dma((VARS,)), dma, dma((VARS,)), dma, dma((VARS,)),
            dma((3,)), dma((3,)),
        ],
        compiler_params=pltpu.CompilerParams(
            collective_id=0, has_side_effects=True, vmem_limit_bytes=60 * 1024 * 1024
        ),
        name="adi_step",
    )(advection, flow_state.reshape(field), *tables)
    return update.reshape(flow_state.shape), rms


def solution(mesh):
    sizes = [mesh.shape[axis] for axis in ("gx", "gy", "gz")]
    return jax.shard_map(
        functools.partial(shards, *sizes),
        mesh=mesh,
        in_specs=(P(None, "gz", "gy", "gx"), P(), P(), P(), P(), P(), P(), P()),
        out_specs=(P(None, "gz", "gy", "gx"), P()),
        check_vma=False,
    )
```

time: 199 us -> 57.4 us (0.29); the launches traced: 196 us -> 56.5 us
  local copies, waits for them, and re-layouts: 57.7 us -> 3.02 us
  Pallas kernels: 0 us -> 52.8 us
  blocking collectives: 33.8 us -> 0 us
  waiting for transfers between devices: 29.6 us -> 0 us
  starting transfers between devices: 27.3 us -> 0 us
  other arithmetic: 24 us -> 0 us
  between operations: 13 us -> 0.65 us
  matrix products: 10.5 us -> 0 us
    pallas_call x0 -> x1, Pallas kernels: none -> 52.8 us  [shards(): pl.pallas_call(functools.partial(kernel, px, py, pz), out_shape=(jax.Shap...]
    all_gather x4 -> x0, blocking collectives: 33.8 us -> none  [collected_together(): both, at, found = (lax.all_gather(jnp.concatenate(lines), axis), 0, {})]
    all_to_all x3 -> x0, waiting for transfers between devices: 29.6 us -> none  [from_everyone(): lax.all_to_all(jnp.broadcast_to(shard[None], (devices, *shard.shape)), ax...]
    all_to_all x3 -> x0, starting transfers between devices: 15.6 us -> none  [from_everyone(): lax.all_to_all(jnp.broadcast_to(shard[None], (devices, *shard.shape)), ax...]
    slice x19 -> x0, local copies, waits for them, and re-layouts: 14.4 us -> none  [the longest x4 4.01 us: line_solve(): lax.slice_in_dim(local_part, 0, 2, axis=line_axis)]
    unnamed x46 -> x4, local copies, waits for them, and re-layouts: 14.9 us -> 3.02 us
    ppermute x6 -> x0, starting transfers between devices: 11.7 us -> none  [the longest x3 6.26 us: padded_2(): lax.ppermute(first, axis, [(b, a) for a, b in up])]
    reduce_sum x5 -> x0, other arithmetic: 10.6 us -> none  [the longest x1 9.21 us: shards(): local_sums = jnp.sum(residual * residual, axis=(1, 2, 3))]
  transfers between devices with their start and end apart: 9 -> 0, of which waited for: 1 -> 0; matrix products, arithmetic and copies ran while one was open for 15% -> 0% of each run, Pallas kernels for 0% -> 0%
where the time goes in v1:
time: 57.4 us; the launch traced here: 56.5 us
  Pallas kernels  52.8 us (92%)
  local copies, waits for them, and re-layouts  3.02 us (5%)
  between operations  0.65 us (1%)
    pallas_call x1, Pallas kernels, shards(): pl.pallas_call(functools.partial(kernel, px, py, pz), out_shape=(jax.Shap...  52.8 us
    unnamed x4, local copies, waits for them, and re-layouts  3.02 us

profile of v1, /device:TPU:1, one launch (start us, length us, event | category | flops | bytes accessed | tf_op | source)
XLA Modules:
  0.0 56.5 jit_solution(7187797706743511664)
XLA Ops:
  0.6 52.8 %adi_step.1 = (f32[5,512,128]{2,1,0:T(8,128)}, f32[5]{0:T(128)}) custom-call(f32[3,5]{1,0:T(4,128)} %adv.1, f32[5,512,128]{2,1,0:T(8,128)} %bitcast.2, f32[5,128,128]{2,1,0:T(8,128)} %inv_x.1, f32[5,16,16]{2,1,0:T(8,128)} %inv_y.1, f32[5,32,32]{2,1,0:T(8,128)} %inv_z.1, f32[5,16,16]{2,1,0:T(8,128)} %red_x.1, f32[5,32,32]{2,1,0:T(8,128)} %red_y.1, ...), custom_call_target="tpu_custom_call" | custom-call | tf_op jit(solution)/shard_map/adi_step/pallas_call | solution.py:456
  53.5 0.0 copy-start
  53.5 2.5 %copy.12 = f32[5,32,16,128]{3,2,1,0:T(8,128)} copy(f32[5,32,16,128]{3,2,1,0:T(8,128)} %bitcast.3) | data formatting | bytes 2621440
  56.0 0.0 copy-done
  56.0 0.5 copy.13
Async XLA Ops:
  53.5 2.5 %copy-start = (f32[5]{0:T(128)S(1)}, f32[5]{0:T(128)}, u32[]{:S(2)}) copy-start(f32[5]{0:T(128)} %get-tuple-element.9) | copy-start | bytes 64

commit v2 on v1

v2 whole, which is shorter than its diff:
```python
import functools

import jax
import jax.numpy as jnp
from jax import lax
from jax.experimental import pallas as pl
from jax.experimental.pallas import tpu as pltpu
from jax.sharding import PartitionSpec as P

VARS, CX, CY, CZ = 5, 128, 16, 32
PLANE = CY
ROWS = CZ * CY
F32, BF16 = jnp.float32, jnp.bfloat16
MESH = pl.DeviceIdType.MESH
NT = (((1,), (1,)), ((), ()))


def iota(shape, dim):
    return lax.broadcasted_iota(jnp.int32, shape, dim)


def log2(n):
    return n.bit_length() - 1


def split(x):
    hi = x.astype(BF16)
    return hi, (x - hi.astype(F32)).astype(BF16)


def dot(a, b):
    return jnp.dot(a, b, preferred_element_type=F32)


def dot_nt(a, b):
    return lax.dot_general(a, b, NT, preferred_element_type=F32)


def mm2(left, right):
    wide = dot(left, jnp.concatenate(split(right), axis=1))
    m, n = left.shape[0] // 2, right.shape[1]
    return (wide[:m, :n] + wide[:m, n:]) + wide[m:, :n]


def nt2(left, right):
    wide = dot_nt(left, right)
    n = right.shape[0] // 2
    return wide[:, :n] + wide[:, n:]


def mm3(left_hi, left_lo, right):
    hi, lo = split(right)
    return dot(left_hi, hi) + (dot(left_hi, lo) + dot(left_lo, hi))


def one_hot(cond):
    return jnp.where(cond, 1.0, 0.0).astype(BF16)


def edge(k, length):
    return jnp.where(k < 2, k, k + (length - 4))


def expand(parts, rows, row_map, cols, col_map):
    n, m = parts[0].shape
    row_i, _ = row_map(iota((rows, n), 0))
    pick_rows = one_hot(row_i == iota((rows, n), 1))
    col_j, _ = col_map(iota((m, cols), 1))
    pick_cols = one_hot(col_j == iota((m, cols), 0))
    _, row_r = row_map(iota((rows, cols), 0))
    _, col_c = col_map(iota((rows, cols), 1))
    keep = row_r == col_c
    return [
        jnp.where(keep, dot(pick_rows, dot(part, pick_cols).astype(BF16)), 0.0).astype(BF16)
        for part in parts
    ]


def coupling(shape, speed, row_of):
    row, col = iota(shape, 0), iota(shape, 1)
    base, k = row_of(row)
    lower, upper = -0.5 * speed - 2.0, 0.5 * speed - 2.0
    out = jnp.where((k == 0) & (col == base - 2), 0.5, 0.0)
    out = out + jnp.where((k == 0) & (col == base - 1), lower, 0.0)
    out = out + jnp.where((k == 1) & (col == base - 1), 0.5, 0.0)
    out = out + jnp.where((k == 2) & (col == base + 4), 0.5, 0.0)
    out = out + jnp.where((k == 3) & (col == base + 4), upper, 0.0)
    return out + jnp.where((k == 3) & (col == base + 5), 0.5, 0.0)


def primitives(u):
    scale = 1.0 / u[0]
    vel = [u[1] * scale, u[2] * scale, u[3] * scale]
    kinetic = 0.5 * (vel[0] * vel[0] + vel[1] * vel[1] + vel[2] * vel[2])
    internal = jnp.maximum(u[4] * scale - kinetic, 0.25)
    return vel, internal, 0.4 * u[0] * internal


def fluxes(u, w, pressure, direction):
    out = [u[1 + direction]]
    for c in range(3):
        moment = u[1 + c] * w
        out.append(moment + pressure if c == direction else moment)
    return out + [(u[4] + pressure) * w]


def kernel(
    px, py, pz,
    tab_adv, flow, *refs,
):
    (
        tab_x, tab_y, tab_z, tab_rx, tab_ry, tab_rz,
        F, rms,
        adv, inv_x, inv_y, inv_z, red_x, red_y, red_z,
        U, PR, FZ, YS, YH, HY, PK, XH, XC, FS, XL, YL, ZL, FG, XR, CT,
        YF, YR1, Y2, YR2, ZF, ZR1, Z2, ZR2, STX, STY, STZ,
        AX, WX, LX, MY, MZ, KY, KZ, SY, SZ,
        in_sem, hs, hr, xs, xrv, ysem, yr1s, y2sem, yr2s, zsem, zr1s, z2sem, zr2s, ss, sr,
    ) = refs
    ix, iy, iz = lax.axis_index("gx"), lax.axis_index("gy"), lax.axis_index("gz")
    zc, yc = CZ // py, CY // pz
    yr, zr = 4 * zc, 4 * yc

    def peer(axis, d):
        me, n = {"gx": (ix, px), "gy": (iy, py), "gz": (iz, pz)}[axis]
        return {axis: (me + d + n) & (n - 1)}

    def remote(src, dst, send, recv, device):
        return pltpu.make_async_remote_copy(
            src_ref=src, dst_ref=dst, send_sem=send, recv_sem=recv,
            device_id=device, device_id_type=MESH,
        )

    def drain(ref, sem):
        pltpu.make_async_copy(ref, ref, sem).wait()

    load = pltpu.make_async_copy(flow, U.at[:, pl.ds(2 * PLANE, ROWS)], in_sem.at[0])
    load.start()
    tables = [
        pltpu.make_async_copy(src, dst, in_sem.at[1 + k])
        for k, (src, dst) in enumerate(zip(
            (tab_adv, tab_x, tab_y, tab_z, tab_rx, tab_ry, tab_rz),
            (adv, inv_x, inv_y, inv_z, red_x, red_y, red_z),
        ))
    ]
    for copy in tables:
        copy.start()
    barrier = pltpu.get_barrier_semaphore()
    for axis, n in (("gz", pz), ("gy", py), ("gx", px)):
        for d in range(1, n):
            pl.semaphore_signal(barrier, inc=1, device_id=peer(axis, d), device_id_type=MESH)
    load.wait()

    def pack_rows(v, carry):
        for r in range(2):
            for t in range(CZ // 8):
                for side, first in ((0, CY - 2), (1, 0)):
                    start = 2 * PLANE + 8 * t * PLANE + first + r
                    YS[side, v, pl.ds(r * CZ + 8 * t, 8), :] = U[v, pl.ds(start, 8, stride=PLANE), :]
        return carry

    lax.fori_loop(0, VARS, pack_rows, 0)
    lane = iota((CY, CX), 1)
    row = iota((CY, CX), 0)

    def pack_lanes(v, carry):
        acc = jnp.zeros((CY, CX), F32)
        for z in range(CZ):
            plane = U[v, pl.ds((2 + z) * PLANE, PLANE), :]
            acc = jnp.where((lane >> 2) == z, pltpu.roll(plane, (4 * z + 2) % CX, 1), acc)
        PK[v] = acc
        return carry

    lax.fori_loop(0, VARS, pack_lanes, 0)

    def plane_primitives(base):
        here = pl.ds(base, PLANE)
        u = [U[v, here, :] for v in range(VARS)]
        vel, internal, pressure = primitives(u)
        PR[0, here, :], PR[1, here, :], PR[2, here, :] = vel[0], vel[1], pressure
        for k, f in enumerate(fluxes(u, vel[2], pressure, 2)[1:]):
            FZ[k, here, :] = f
        return vel, internal

    def first_pass(step, top):
        for k in range(2):
            base = pl.multiple_of(2 * PLANE + (2 * step + k) * PLANE, PLANE)
            vel, internal = plane_primitives(base)
            speed = jnp.abs(vel[0]) + jnp.abs(vel[1]) + jnp.abs(vel[2]) + jnp.sqrt(3.0 * 1.4 * 0.4 * internal)
            top = jnp.maximum(top, speed)
        return top

    top = lax.fori_loop(0, CZ // 2, first_pass, jnp.zeros((CY, CX), F32))

    for copy in tables:
        copy.wait()
    high = lax.Precision.HIGHEST

    def exact_dot(a, b):
        return jnp.dot(a, b, precision=high, preferred_element_type=F32)

    def columns(table, length):
        shape = (length, 4 * CX)
        pick = one_hot(iota(shape, 0) == edge(iota(shape, 1) >> 7, length))
        hi, lo = split(table)
        return dot(hi, pick) + dot(lo, pick)

    def build_first(v, carry):
        hi, lo = split(inv_x[v])
        AX[v] = jnp.concatenate([jnp.concatenate([hi, hi], 1), jnp.concatenate([lo, lo], 1)], 0)
        col = iota((CX, CX), 1)
        pick = one_hot(((col >> 2) == v) & (iota((CX, CX), 0) == edge(col & 3, CX)))
        hi, lo = dot(hi, pick).astype(BF16), dot(lo, pick).astype(BF16)
        WX[v] = jnp.concatenate([jnp.concatenate([hi, hi], 1), jnp.concatenate([lo, lo], 1)], 0)

        pick = one_hot(iota((CY, CX), 0) == (iota((CY, CX), 1) & (CY - 1)))
        for part, table in enumerate(split(inv_y[v])):
            spread = dot(table, pick)
            for z in range(8):
                block = jnp.where((lane >> 4) == z, spread, 0.0)
                MY[v, part * CX + 16 * z : part * CX + 16 * z + 16, :] = block.astype(BF16)
        return carry

    lax.fori_loop(0, VARS, build_first, 0)
    for t in range(3):
        acc = jnp.zeros((8, 8 * px), F32)
        for v in (2 * t, 2 * t + 1):
            if v == VARS:
                continue
            own = coupling((8, 4 * px), adv[0, v], lambda r: (4 * ix, r & 3))
            rows = exact_dot(own, red_x[v])
            r, c = iota((4 * px, 8 * px), 0), iota((4 * px, 8 * px), 1)
            wide = exact_dot(rows, jnp.where(r == ((c >> 3) << 2) + (c & 3), 1.0, 0.0))
            r, c = iota((8, 8 * px), 0), iota((8, 8 * px), 1)
            acc = acc + jnp.where(((r >> 2) == v - 2 * t) & (((c >> 2) & 1) == v - 2 * t), wide, 0.0)
        LX[t] = acc

    pl.semaphore_wait(barrier, px + py + pz - 3)
    last = 2 * PLANE + ROWS
    halos = [
        remote(flow.at[:, pl.ds(ROWS - 2 * PLANE, 2 * PLANE)], U.at[:, pl.ds(0, 2 * PLANE)],
               hs.at[0], hr.at[0], peer("gz", 1)),
        remote(flow.at[:, pl.ds(0, 2 * PLANE)], U.at[:, pl.ds(last, 2 * PLANE)],
               hs.at[1], hr.at[1], peer("gz", -1)),
        remote(YS.at[0], YH.at[0], hs.at[2], hr.at[2], peer("gy", 1)),
        remote(YS.at[1], YH.at[1], hs.at[3], hr.at[3], peer("gy", -1)),
        remote(PK, XH.at[0], hs.at[4], hr.at[4], peer("gx", 1)),
        remote(PK, XH.at[1], hs.at[5], hr.at[5], peer("gx", -1)),
    ]
    for copy in halos:
        copy.start()

    def build_second(v, carry):
        SY[v] = columns(inv_y[v], CY)

        wide = iota((CZ, 8 * CZ), 1)
        pick = one_hot(iota((CZ, 8 * CZ), 0) == (wide >> 3))
        r, c = iota((16, 8 * CZ), 0), iota((16, 8 * CZ), 1)
        keep, first = (r & 7) == (c & 7), r < 8
        for part, table in enumerate(split(inv_z[v])):
            spread = dot(table, pick)
            for k in range(CZ // 2):
                pair = [jnp.broadcast_to(spread[z : z + 1], (16, 8 * CZ)) for z in (2 * k, 2 * k + 1)]
                block = jnp.where(keep, jnp.where(first, pair[0], pair[1]), 0.0)
                MZ[v, part * 256 + 16 * k : part * 256 + 16 * k + 16, :] = block.astype(BF16)
        SZ[v] = columns(inv_z[v], CZ)

        def reduced(red, n, speed):
            g = coupling((4 * n, 4 * n), speed, lambda r: ((r >> 2) << 2, r & 3))
            return split(exact_dot(g, red))

        y_side = lambda r: (r >> log2(zc), r & (zc - 1))
        hi, lo = expand(reduced(red_y[v], py, adv[1, v]), 4 * CZ, y_side, 4 * CZ, y_side)
        KY[v, 0:CX, :], KY[v, CX : 2 * CX, :] = hi, lo
        z_side = lambda r: (r >> log2(yc), r & (yc - 1))
        KZ[0, v], KZ[1, v] = expand(reduced(red_z[v], pz, adv[2, v]), 4 * CY, z_side, 4 * CY, z_side)
        return carry

    lax.fori_loop(0, VARS, build_second, 0)
    for copy in halos:
        copy.wait_recv()
    plane_primitives(PLANE)
    plane_primitives(last)
    for side in range(2):
        near1, near2 = pl.ds((1 - side) * CZ, CZ), pl.ds(side * CZ, CZ)
        u = [YH[side, v, near1, :] for v in range(VARS)]
        vel, _, pressure = primitives(u)
        half = 0.5 - side
        for v, f in enumerate(fluxes(u, vel[1], pressure, 1)):
            HY[2 * side, v] = -0.0625 * u[v]
            HY[2 * side + 1, v] = 0.25 * u[v] + half * f - 0.0625 * YH[side, v, near2, :]
    j = lane & 3
    near = [jnp.where(j < 2, XH[0, v], XH[1, v]) for v in range(VARS)]
    mine = [PK[v] for v in range(VARS)]
    vel, _, pressure = primitives(near)
    near_flux = fluxes(near, vel[0], pressure, 0)
    vel, _, pressure = primitives(mine)
    mine_flux = fluxes(mine, vel[0], pressure, 0)
    for v in range(VARS):
        du, df = near[v] - mine[v], near_flux[v] - mine_flux[v]
        far = -0.0625 * jnp.where(j < 2, pltpu.roll(du, CX - 2, 1), pltpu.roll(du, 2, 1))
        right = pltpu.roll(-0.5 * df + 0.25 * du, CX - 1, 1)
        left = pltpu.roll(0.5 * df + 0.25 * du, 1, 1)
        XC[v] = far + jnp.where(j == 1, right, 0.0) + jnp.where(j == 2, left, 0.0)

    ends = ((lane + 2) & (CX - 1)) < 4
    bottom, ceiling = row == 0, row == CY - 1

    def residual_plane(z, sums):
        base = pl.multiple_of(2 * PLANE + z * PLANE, PLANE)

        def at(ref, k, step):
            return ref[k, pl.ds(base + step * PLANE, PLANE), :]

        u = [at(U, v, 0) for v in range(VARS)]
        pressure = at(PR, 2, 0)
        x_flux = fluxes(u, at(PR, 0, 0), pressure, 0)
        y_flux = fluxes(u, at(PR, 1, 0), pressure, 1)
        done = []
        for v in range(VARS):
            f = u[v]
            ahead, behind = at(U, v, 1), at(U, v, -1)
            if v == 0:
                slope = at(U, 3, 1) - at(U, 3, -1)
            else:
                slope = at(FZ, v - 1, 1) - at(FZ, v - 1, -1)

            def halo(k):
                return jnp.broadcast_to(HY[k, v, pl.ds(z, 1), :], (CY, CX))

            far, quarter = -0.0625 * f, 0.25 * f
            half = 0.5 * y_flux[v]
            up = quarter + half + jnp.where(bottom, halo(0), pltpu.roll(far, 1, 0))
            down = quarter - half + jnp.where(ceiling, halo(2), pltpu.roll(far, CY - 1, 0))
            r = jnp.where(bottom, halo(1), pltpu.roll(up, 1, 0))
            r = r + jnp.where(ceiling, halo(3), pltpu.roll(down, CY - 1, 0))
            half = 0.5 * x_flux[v]
            up = quarter + half + pltpu.roll(far, 1, 1)
            down = quarter - half + pltpu.roll(far, CX - 1, 1)
            r = r + (pltpu.roll(up, 1, 1) + pltpu.roll(down, CX - 1, 1))
            fix = jnp.where(ends, pltpu.roll(XC[v], (2 * CX - 2 - 4 * z) & (CX - 1), 1), 0.0)
            r = r + (0.25 * (ahead + behind) - 0.5 * slope)
            r = r + (fix - 0.0625 * (at(U, v, 2) + at(U, v, -2))) - 1.125 * f
            F[v, pl.ds(pl.multiple_of(z * PLANE, PLANE), PLANE), :] = r
            done.append(sums[v] + r * r)
        return done

    def second_pass(step, sums):
        for k in range(2):
            sums = residual_plane(2 * step + k, sums)
        return sums

    sums = lax.fori_loop(0, CZ // 2, second_pass, [jnp.zeros((CY, CX), F32)] * VARS)

    row8 = iota((8, 4 * CX), 0)
    for t in range(3):
        pair = []
        for v in (2 * t, 2 * t + 1):
            if v == VARS:
                pair.append(jnp.zeros((8, ROWS), F32))
                continue
            tile = jnp.where(iota((8, CX), 0) < 2, inv_x[v, 0:8, :], pltpu.roll(inv_x[v, CX - 8 : CX, :], 4, 0))
            if v & 1:
                tile = pltpu.roll(tile, 4, 0)
            FS[v] = jnp.concatenate(split(F[v]), axis=1)
            hi, lo = split(tile)
            left = jnp.concatenate([jnp.concatenate([hi, hi], 1), jnp.concatenate([lo, lo], 1)], 0)
            both = dot_nt(left, FS[v])
            pair.append(both[0:8] + both[8:16])
        XR[t, ix] = jnp.where(row8 < 4, pair[0], pair[1])
    for d in range(1, px):
        remote(XR.at[:, ix], XR.at[:, ix], xs, xrv, peer("gx", d)).start()

    stat_row = iota((8, CX), 0)
    tile = jnp.where(stat_row == VARS, jnp.max(top), 0.0)
    for v in range(VARS):
        tile = jnp.where(stat_row == v, jnp.sum(sums[v]), tile)
    STX[ix] = tile
    for d in range(1, px):
        remote(STX.at[ix], STX.at[ix], ss.at[0], sr.at[0], peer("gx", d)).start()

    def combine(ref, n):
        total = ref[0]
        for k in range(1, n):
            total = jnp.where(stat_row == VARS, jnp.maximum(total, ref[k]), total + ref[k])
        return total

    def local_x(v, carry):
        XL[v] = nt2(FS[v], AX[v])
        return carry

    lax.fori_loop(0, VARS, local_x, 0)

    drain(XR.at[:, pl.ds(0, px - 1)], xrv)
    factors = [mm3(*split(LX[t]), XR[t].reshape(8 * px, ROWS)) for t in range(3)]
    factors = jnp.concatenate(factors + [jnp.zeros((CX - 24, ROWS), F32)], axis=0).T
    CT[...] = jnp.concatenate(split(factors), axis=1)

    def exchange(axis, me, n, rows, src, dst, v, send, recv):
        mine = pl.ds(pl.multiple_of(me * rows, rows), rows)
        for d in range(1, n):
            to = peer(axis, d)
            there = pl.ds(pl.multiple_of(to[axis] * rows, rows), rows)
            remote(src.at[v, there], dst.at[v, mine], send, recv, to).start()
        dst[v, mine, :] = src[v, mine, :]

    def local_y(v, carry):
        field = XL[v] - nt2(CT[...], WX[v])
        for g in range(4):
            here = slice(128 * g, 128 * g + 128)
            YL[v, here, :] = mm2(MY[v], field[here])
        for k, y in enumerate((0, 1, CY - 2, CY - 1)):
            for t in range(zc):
                lines = YL[v, pl.ds(8 * t * PLANE + y, 8, stride=PLANE), :]
                YF[v, pl.ds(zc * k + t, 8, stride=yr), :] = lines
        exchange("gy", iy, py, yr, YF, YR1, v, ysem, yr1s.at[v])
        return carry

    lax.fori_loop(0, VARS, local_y, 0)
    drain(STX.at[pl.ds(0, px - 1)], sr.at[0])
    STY[iy] = combine(STX, px)
    for d in range(1, py):
        remote(STY.at[iy], STY.at[iy], ss.at[1], sr.at[1], peer("gy", d)).start()

    def reduced_y(v, carry):
        drain(YR1.at[v, pl.ds(0, (py - 1) * yr)], yr1s.at[v])
        Y2[v] = mm2(KY[v], YR1[v])
        exchange("gy", iy, py, yr, Y2, YR2, v, y2sem, yr2s.at[v])
        return carry

    lax.fori_loop(0, VARS, reduced_y, 0)
    drain(STY.at[pl.ds(0, py - 1)], sr.at[1])
    STZ[iz] = combine(STY, py)
    for d in range(1, pz):
        remote(STZ.at[iz], STZ.at[iz], ss.at[2], sr.at[2], peer("gz", d)).start()

    def local_z(v, carry):
        drain(YR2.at[v, pl.ds(0, (py - 1) * yr)], yr2s.at[v])
        column = [SY[v, :, CX * k : CX * k + CX] for k in range(4)]
        for z in range(CZ):
            field = YL[v, z * PLANE : z * PLANE + PLANE, :]
            for k in range(4):
                line = (z & 7) * yr + zc * k + (z >> 3)
                field = field - column[k] * jnp.broadcast_to(YR2[v, line : line + 1, :], (CY, CX))
            FG[0, 8 * z : 8 * z + 8, :] = field[0:8]
            FG[1, 8 * z : 8 * z + 8, :] = field[8:16]
        for g in range(2):
            solved = mm2(MZ[v], FG[g])
            for z in range(CZ):
                ZL[v, z * PLANE + 8 * g : z * PLANE + 8 * g + 8, :] = solved[8 * z : 8 * z + 8]
            for k, z in enumerate((0, 1, CZ - 2, CZ - 1)):
                ZF[v, pl.ds(yc * k + g, 8, stride=zr), :] = solved[8 * z : 8 * z + 8]
        exchange("gz", iz, pz, zr, ZF, ZR1, v, zsem, zr1s.at[v])
        return carry

    lax.fori_loop(0, VARS, local_z, 0)

    def reduced_z(v, carry):
        drain(ZR1.at[v, pl.ds(0, (pz - 1) * zr)], zr1s.at[v])
        Z2[v] = mm3(KZ[0, v], KZ[1, v], ZR1[v])
        exchange("gz", iz, pz, zr, Z2, ZR2, v, z2sem, zr2s.at[v])
        return carry

    lax.fori_loop(0, VARS, reduced_z, 0)
    drain(STZ.at[pl.ds(0, pz - 1)], sr.at[2])
    stats = combine(STZ, pz)
    step = 8000.0 / stats[VARS : VARS + 1]
    rms[...] = jnp.sqrt(stats / float(px * py * pz * ROWS * CX))

    def finish(v, carry):
        drain(ZR2.at[v, pl.ds(0, (pz - 1) * zr)], zr2s.at[v])
        factor = [[ZR2[v, pl.ds(yc * k + g, 8, stride=zr), :] for g in range(2)] for k in range(4)]
        for z in range(CZ):
            weight = [jnp.broadcast_to(SZ[v, z : z + 1, CX * k : CX * k + CX], (8, CX)) for k in range(4)]
            for g in range(2):
                here = slice(z * PLANE + 8 * g, z * PLANE + 8 * g + 8)
                total = ZL[v, here, :]
                for k in range(4):
                    total = total - weight[k] * factor[k][g]
                F[v, here, :] = step * total
        return carry

    lax.fori_loop(0, VARS, finish, 0)
    for copy in halos:
        copy.wait_send()
    drain(XR.at[:, pl.ds(0, px - 1)], xs)
    drain(STX.at[pl.ds(0, px - 1)], ss.at[0])
    drain(STY.at[pl.ds(0, py - 1)], ss.at[1])
    drain(STZ.at[pl.ds(0, pz - 1)], ss.at[2])
    drain(YF.at[:, pl.ds(0, (py - 1) * yr)], ysem)
    drain(Y2.at[:, pl.ds(0, (py - 1) * yr)], y2sem)
    drain(ZF.at[:, pl.ds(0, (pz - 1) * zr)], zsem)
    drain(Z2.at[:, pl.ds(0, (pz - 1) * zr)], z2sem)


def shards(px, py, pz, flow_state, advection, *tables):
    vmem = pl.BlockSpec(memory_space=pltpu.VMEM)
    hbm = pl.BlockSpec(memory_space=pltpu.HBM)
    f32 = lambda *shape: pltpu.VMEM(shape, F32)
    b16 = lambda *shape: pltpu.VMEM(shape, BF16)
    dma = pltpu.SemaphoreType.DMA
    field = (VARS, ROWS, CX)
    padded_rows = ROWS + 4 * PLANE
    y_face, z_face = (VARS, 4 * CZ, CX), (VARS, 4 * CY, CX)
    update, rms = pl.pallas_call(
        functools.partial(kernel, px, py, pz),
        out_shape=(jax.ShapeDtypeStruct(field, F32), jax.ShapeDtypeStruct((8, CX), F32)),
        in_specs=[hbm] * 8,
        out_specs=(vmem, vmem),
        scratch_shapes=[
            pltpu.SMEM(advection.shape, F32), *[f32(*table.shape) for table in tables],
            f32(VARS, padded_rows, CX), f32(3, padded_rows, CX), f32(4, padded_rows, CX),
            f32(2, VARS, 2 * CZ, CX), f32(2, VARS, 2 * CZ, CX), f32(4, VARS, CZ, CX),
            f32(VARS, CY, CX), f32(2, VARS, CY, CX), f32(VARS, CY, CX),
            b16(VARS, ROWS, 2 * CX), f32(*field), f32(*field), f32(*field), f32(2, 256, CX),
            f32(3, px, 8, ROWS), b16(ROWS, 2 * CX),
            *[f32(*y_face)] * 4, *[f32(*z_face)] * 4,
            f32(px, 8, CX), f32(py, 8, CX), f32(pz, 8, CX),
            b16(VARS, 2 * CX, 2 * CX), b16(VARS, 2 * CX, 2 * CX), f32(3, 8, 8 * px),
            b16(VARS, 2 * CX, CX), b16(VARS, 512, 256),
            b16(VARS, 8 * CZ, 4 * CZ), b16(2, VARS, 4 * CY, 4 * CY),
            f32(VARS, CY, 4 * CX), f32(VARS, CZ, 4 * CX),
            dma((8,)), dma((6,)), dma((6,)), dma, dma,
            dma, dma((VARS,)), dma, dma((VARS,)), dma, dma((VARS,)), dma, dma((VARS,)),
            dma((3,)), dma((3,)),
        ],
        compiler_params=pltpu.CompilerParams(
            collective_id=0, has_side_effects=True, vmem_limit_bytes=32 * 1024 * 1024
        ),
        name="adi_step",
    )(*[pltpu.with_memory_space_constraint(x, pltpu.HBM) for x in (advection, flow_state.reshape(field), *tables)])
    return update.reshape(flow_state.shape), rms[:VARS, 0]


def solution(mesh):
    sizes = [mesh.shape[axis] for axis in ("gx", "gy", "gz")]
    return jax.shard_map(
        functools.partial(shards, *sizes),
        mesh=mesh,
        in_specs=(P(None, "gz", "gy", "gx"), P(), P(), P(), P(), P(), P(), P()),
        out_specs=(P(None, "gz", "gy", "gx"), P()),
        check_vma=False,
    )
```

time: 57.4 us -> 47.4 us (0.83); the launches traced: 56.5 us -> 47.3 us
  Pallas kernels: 52.8 us -> 45 us
  local copies, waits for them, and re-layouts: 3.02 us -> 1.68 us
    pallas_call x1, Pallas kernels: 52.8 us -> 45 us  [shards(): pl.pallas_call(functools.partial(kernel, px, py, pz), out_shape=(jax.Shap...]
    unnamed x4 -> x1, local copies, waits for them, and re-layouts: 3.02 us -> 1.06 us
    slice x0 -> x1, local copies, waits for them, and re-layouts: none -> 0.63 us  [shards(): return (update.reshape(flow_state.shape), rms[:VARS, 0])]
where the time goes in v2:
time: 47.4 us; the launch traced here: 47.3 us
  Pallas kernels  45 us (95%)
  local copies, waits for them, and re-layouts  1.68 us (4%)
  between operations  0.64 us (1%)
    pallas_call x1, Pallas kernels, shards(): pl.pallas_call(functools.partial(kernel, px, py, pz), out_shape=(jax.Shap...  45 us
    unnamed x1, local copies, waits for them, and re-layouts  1.06 us

profile of v2, /device:TPU:1, one launch (start us, length us, event | category | flops | bytes accessed | tf_op | source)
XLA Modules:
  0.0 47.3 jit_solution(601391533532608389)
XLA Ops:
  0.6 45.0 %adi_step.1 = (f32[5,512,128]{2,1,0:T(8,128)S(1)}, f32[8,128]{1,0:T(8,128)S(1)}) custom-call(f32[3,5]{1,0:T(4,128)} %tab_adv.1, f32[5,512,128]{2,1,0:T(8,128)} %bitcast.3, f32[5,128,128]{2,1,0:T(8,128)} %refs_0_.1, f32[5,16,16]{2,1,0:T(8,128)} %refs_1_.1, f32[5,32,32]{2,1,0:T(8,128)} %refs_2_.1, f32[5,16,16]{2,1,0:T(8,128)} %refs_3_.1, ...), custom_call_target="tpu_custom_call" | custom-call | tf_op jit(solution)/shard_map/adi_step/pallas_call | solution.py:505
  45.6 0.6 %slice_reduce_fusion = f32[5]{0:T(128)} fusion(f32[8,128]{1,0:T(8,128)S(1)} %get-tuple-element.5), kind=kLoop, calls=%fused_computation | loop fusion | bytes 40 | tf_op jit(solution)/shard_map/slice | solution.py:532
  46.3 1.1 %copy.11 = f32[5,32,16,128]{3,2,1,0:T(8,128)} copy(f32[5,32,16,128]{3,2,1,0:T(8,128)S(1)} %bitcast.2) | data formatting | bytes 2621440

commit v3 on v2

v3 whole, which is shorter than its diff:
```python
import functools

import jax
import jax.numpy as jnp
from jax import lax
from jax.experimental import pallas as pl
from jax.experimental.pallas import tpu as pltpu
from jax.sharding import PartitionSpec as P

VARS, CX, CY, CZ = 5, 128, 16, 32
PLANE = CY
ROWS = CZ * CY
F32, BF16 = jnp.float32, jnp.bfloat16
MESH = pl.DeviceIdType.MESH
NT = (((1,), (1,)), ((), ()))


def iota(shape, dim):
    return lax.broadcasted_iota(jnp.int32, shape, dim)


def log2(n):
    return n.bit_length() - 1


def split(x):
    hi = x.astype(BF16)
    return hi, (x - hi.astype(F32)).astype(BF16)


def dot(a, b):
    return jnp.dot(a, b, preferred_element_type=F32)


def dot_nt(a, b):
    return lax.dot_general(a, b, NT, preferred_element_type=F32)


def mm2(left, right):
    wide = dot(left, jnp.concatenate(split(right), axis=1))
    m, n = left.shape[0] // 2, right.shape[1]
    return (wide[:m, :n] + wide[:m, n:]) + wide[m:, :n]


def nt2(left, right):
    wide = dot_nt(left, right)
    n = right.shape[0] // 2
    return wide[:, :n] + wide[:, n:]


def mm3(left_hi, left_lo, right):
    hi, lo = split(right)
    return dot(left_hi, hi) + (dot(left_hi, lo) + dot(left_lo, hi))


def one_hot(cond):
    return jnp.where(cond, 1.0, 0.0).astype(BF16)


def edge(k, length):
    return jnp.where(k < 2, k, k + (length - 4))


def expand(parts, rows, row_map, cols, col_map):
    n, m = parts[0].shape
    row_i, _ = row_map(iota((rows, n), 0))
    pick_rows = one_hot(row_i == iota((rows, n), 1))
    col_j, _ = col_map(iota((m, cols), 1))
    pick_cols = one_hot(col_j == iota((m, cols), 0))
    _, row_r = row_map(iota((rows, cols), 0))
    _, col_c = col_map(iota((rows, cols), 1))
    keep = row_r == col_c
    return [
        jnp.where(keep, dot(pick_rows, dot(part, pick_cols).astype(BF16)), 0.0).astype(BF16)
        for part in parts
    ]


def coupling(shape, speed, row_of):
    row, col = iota(shape, 0), iota(shape, 1)
    base, k = row_of(row)
    lower, upper = -0.5 * speed - 2.0, 0.5 * speed - 2.0
    out = jnp.where((k == 0) & (col == base - 2), 0.5, 0.0)
    out = out + jnp.where((k == 0) & (col == base - 1), lower, 0.0)
    out = out + jnp.where((k == 1) & (col == base - 1), 0.5, 0.0)
    out = out + jnp.where((k == 2) & (col == base + 4), 0.5, 0.0)
    out = out + jnp.where((k == 3) & (col == base + 4), upper, 0.0)
    return out + jnp.where((k == 3) & (col == base + 5), 0.5, 0.0)


def primitives(u):
    scale = 1.0 / u[0]
    vel = [u[1] * scale, u[2] * scale, u[3] * scale]
    kinetic = 0.5 * (vel[0] * vel[0] + vel[1] * vel[1] + vel[2] * vel[2])
    internal = jnp.maximum(u[4] * scale - kinetic, 0.25)
    return vel, internal, 0.4 * u[0] * internal


def fluxes(u, w, pressure, direction):
    out = [u[1 + direction]]
    for c in range(3):
        moment = u[1 + c] * w
        out.append(moment + pressure if c == direction else moment)
    return out + [(u[4] + pressure) * w]


def kernel(
    px, py, pz,
    tab_adv, flow, *refs,
):
    (
        tab_x, tab_y, tab_z, tab_rx, tab_ry, tab_rz,
        F, rms,
        adv, inv_x, inv_y, inv_z, red_x, red_y, red_z,
        U, PR, FZ, YS, YH, HY, PK, XH, XC, FS, XL, G, FG, XR, CT,
        YF, YR1, Y2, YR2, ZF, ZR1, Z2, ZR2, E, ER, CF, STX, STY, STZ,
        AX, WX, LX, MY, MZ, KY, KZ, SY, SZ,
        in_sem, hs, hr, xs, xrv, ysem, yr1s, y2sem, yr2s, zsem, zr1s, z2sem, zr2s, es, ers, ss, sr,
    ) = refs
    ix, iy, iz = lax.axis_index("gx"), lax.axis_index("gy"), lax.axis_index("gz")
    zc, yc = CZ // py, CY // pz
    yr, zr = 4 * zc, 4 * yc

    def peer(axis, d):
        me, n = {"gx": (ix, px), "gy": (iy, py), "gz": (iz, pz)}[axis]
        return {axis: (me + d + n) & (n - 1)}

    def remote(src, dst, send, recv, device):
        return pltpu.make_async_remote_copy(
            src_ref=src, dst_ref=dst, send_sem=send, recv_sem=recv,
            device_id=device, device_id_type=MESH,
        )

    def drain(ref, sem):
        pltpu.make_async_copy(ref, ref, sem).wait()

    load = pltpu.make_async_copy(flow, U.at[:, pl.ds(2 * PLANE, ROWS)], in_sem.at[0])
    load.start()
    tables = [
        pltpu.make_async_copy(src, dst, in_sem.at[1 + k])
        for k, (src, dst) in enumerate(zip(
            (tab_adv, tab_x, tab_y, tab_z, tab_rx, tab_ry, tab_rz),
            (adv, inv_x, inv_y, inv_z, red_x, red_y, red_z),
        ))
    ]
    for copy in tables:
        copy.start()
    barrier = pltpu.get_barrier_semaphore()
    for axis, n in (("gz", pz), ("gy", py), ("gx", px)):
        for d in range(1, n):
            pl.semaphore_signal(barrier, inc=1, device_id=peer(axis, d), device_id_type=MESH)
    load.wait()

    def pack_rows(v, carry):
        for r in range(2):
            for t in range(CZ // 8):
                for side, first in ((0, CY - 2), (1, 0)):
                    start = 2 * PLANE + 8 * t * PLANE + first + r
                    YS[side, v, pl.ds(r * CZ + 8 * t, 8), :] = U[v, pl.ds(start, 8, stride=PLANE), :]
        return carry

    lax.fori_loop(0, VARS, pack_rows, 0, unroll=True)
    lane = iota((CY, CX), 1)
    row = iota((CY, CX), 0)

    def pack_lanes(v, carry):
        acc = jnp.zeros((CY, CX), F32)
        for z in range(CZ):
            plane = U[v, pl.ds((2 + z) * PLANE, PLANE), :]
            acc = jnp.where((lane >> 2) == z, pltpu.roll(plane, (4 * z + 2) % CX, 1), acc)
        PK[v] = acc
        return carry

    lax.fori_loop(0, VARS, pack_lanes, 0, unroll=True)

    pl.semaphore_wait(barrier, px + py + pz - 3)
    last = 2 * PLANE + ROWS
    halos = [
        remote(flow.at[:, pl.ds(ROWS - 2 * PLANE, 2 * PLANE)], U.at[:, pl.ds(0, 2 * PLANE)],
               hs.at[0], hr.at[0], peer("gz", 1)),
        remote(flow.at[:, pl.ds(0, 2 * PLANE)], U.at[:, pl.ds(last, 2 * PLANE)],
               hs.at[1], hr.at[1], peer("gz", -1)),
        remote(YS.at[0], YH.at[0], hs.at[2], hr.at[2], peer("gy", 1)),
        remote(YS.at[1], YH.at[1], hs.at[3], hr.at[3], peer("gy", -1)),
        remote(PK, XH.at[0], hs.at[4], hr.at[4], peer("gx", 1)),
        remote(PK, XH.at[1], hs.at[5], hr.at[5], peer("gx", -1)),
    ]
    for copy in halos:
        copy.start()

    def plane_primitives(base):
        here = pl.ds(base, PLANE)
        u = [U[v, here, :] for v in range(VARS)]
        vel, internal, pressure = primitives(u)
        PR[0, here, :], PR[1, here, :], PR[2, here, :] = vel[0], vel[1], pressure
        for k, f in enumerate(fluxes(u, vel[2], pressure, 2)[1:]):
            FZ[k, here, :] = f
        return vel, internal

    def first_pass(step, top):
        for k in range(2):
            base = pl.multiple_of(2 * PLANE + (2 * step + k) * PLANE, PLANE)
            vel, internal = plane_primitives(base)
            speed = jnp.abs(vel[0]) + jnp.abs(vel[1]) + jnp.abs(vel[2]) + jnp.sqrt(3.0 * 1.4 * 0.4 * internal)
            top = jnp.maximum(top, speed)
        return top

    top = lax.fori_loop(0, CZ // 2, first_pass, jnp.zeros((CY, CX), F32))

    for copy in tables:
        copy.wait()
    def exact_dot(a, b):
        return mm3(*split(a), b)

    def columns(table, length):
        shape = (length, 4 * CX)
        pick = one_hot(iota(shape, 0) == edge(iota(shape, 1) >> 7, length))
        hi, lo = split(table)
        return dot(hi, pick) + dot(lo, pick)

    def build_first(v, carry):
        hi, lo = split(inv_x[v])
        AX[v] = jnp.concatenate([jnp.concatenate([hi, hi], 1), jnp.concatenate([lo, lo], 1)], 0)
        col = iota((CX, CX), 1)
        pick = one_hot(((col >> 2) == (v & 1)) & (iota((CX, CX), 0) == edge(col & 3, CX)))
        hi, lo = dot(hi, pick).astype(BF16), dot(lo, pick).astype(BF16)
        WX[v] = jnp.concatenate([jnp.concatenate([hi, hi], 1), jnp.concatenate([lo, lo], 1)], 0)

        pick = one_hot(iota((CY, CX), 0) == (iota((CY, CX), 1) & (CY - 1)))
        for part, table in enumerate(split(inv_y[v])):
            spread = dot(table, pick)
            for z in range(8):
                block = jnp.where((lane >> 4) == z, spread, 0.0)
                MY[v, part * CX + 16 * z : part * CX + 16 * z + 16, :] = block.astype(BF16)
        return carry

    lax.fori_loop(0, VARS, build_first, 0, unroll=True)
    for t in range(3):
        acc = jnp.zeros((8, 8 * px), F32)
        for v in (2 * t, 2 * t + 1):
            if v == VARS:
                continue
            own = coupling((8, 4 * px), adv[0, v], lambda r: (4 * ix, r & 3))
            rows = exact_dot(own, red_x[v])
            r, c = iota((4 * px, 8 * px), 0), iota((4 * px, 8 * px), 1)
            wide = exact_dot(rows, jnp.where(r == ((c >> 3) << 2) + (c & 3), 1.0, 0.0))
            r, c = iota((8, 8 * px), 0), iota((8, 8 * px), 1)
            acc = acc + jnp.where(((r >> 2) == v - 2 * t) & (((c >> 2) & 1) == v - 2 * t), wide, 0.0)
        LX[t] = acc

    ends = ((lane + 2) & (CX - 1)) < 4

    def residual_plane(group, z):
        base = pl.multiple_of(2 * PLANE + z * PLANE, PLANE)

        def at(ref, k, step):
            return ref[k, pl.ds(base + step * PLANE, PLANE), :]

        u = [at(U, v, 0) for v in range(VARS)]
        pressure = at(PR, 2, 0)
        x_flux = fluxes(u, at(PR, 0, 0), pressure, 0)
        y_flux = fluxes(u, at(PR, 1, 0), pressure, 1)
        for v in group:
            f = u[v]
            ahead, behind = at(U, v, 1), at(U, v, -1)
            if v == 0:
                slope = at(U, 3, 1) - at(U, 3, -1)
            else:
                slope = at(FZ, v - 1, 1) - at(FZ, v - 1, -1)

            far, quarter = -0.0625 * f, 0.25 * f
            half = 0.5 * y_flux[v]
            up = quarter + half + pltpu.roll(far, 1, 0)
            down = quarter - half + pltpu.roll(far, CY - 1, 0)
            r = pltpu.roll(up, 1, 0) + pltpu.roll(down, CY - 1, 0)
            half = 0.5 * x_flux[v]
            up = quarter + half + pltpu.roll(far, 1, 1)
            down = quarter - half + pltpu.roll(far, CX - 1, 1)
            r = r + (pltpu.roll(up, 1, 1) + pltpu.roll(down, CX - 1, 1))
            r = r + (0.25 * (ahead + behind) - 0.5 * slope)
            r = r - 0.0625 * (at(U, v, 2) + at(U, v, -2)) - 1.125 * f
            F[v, pl.ds(pl.multiple_of(z * PLANE, PLANE), PLANE), :] = r

    def interior(step, carry):
        for k in range(2):
            residual_plane(range(VARS), 2 + 2 * step + k)
        return carry

    lax.fori_loop(0, (CZ - 4) // 2, interior, 0)
    def build_z(v, carry):
        wide = iota((CZ, 8 * CZ), 1)
        pick = one_hot(iota((CZ, 8 * CZ), 0) == (wide >> 3))
        r, c = iota((16, 8 * CZ), 0), iota((16, 8 * CZ), 1)
        keep, first = (r & 7) == (c & 7), r < 8
        for part, table in enumerate(split(inv_z[v])):
            spread = dot(table, pick)
            for k in range(CZ // 2):
                pair = [jnp.broadcast_to(spread[z : z + 1], (16, 8 * CZ)) for z in (2 * k, 2 * k + 1)]
                block = jnp.where(keep, jnp.where(first, pair[0], pair[1]), 0.0)
                MZ[v, part * 256 + 16 * k : part * 256 + 16 * k + 16, :] = block.astype(BF16)
        return carry

    lax.fori_loop(0, VARS, build_z, 0, unroll=True)
    for copy in halos:
        copy.wait_recv()
    plane_primitives(PLANE)
    plane_primitives(last)
    for side in range(2):
        half = 0.5 - side
        parts = []
        for ref, which in ((YH, side), (YS, side)):
            near, far = pl.ds((1 - side) * CZ, CZ), pl.ds(side * CZ, CZ)
            u = [ref[which, v, near, :] for v in range(VARS)]
            vel, _, pressure = primitives(u)
            parts.append([
                (-0.0625 * u[v], 0.25 * u[v] + half * f - 0.0625 * ref[which, v, far, :])
                for v, f in enumerate(fluxes(u, vel[1], pressure, 1))
            ])
        for v in range(VARS):
            for k in range(2):
                HY[2 * side + k, v] = parts[0][v][k] - parts[1][v][k]
    j = lane & 3
    near = [jnp.where(j < 2, XH[0, v], XH[1, v]) for v in range(VARS)]
    mine = [PK[v] for v in range(VARS)]
    vel, _, pressure = primitives(near)
    near_flux = fluxes(near, vel[0], pressure, 0)
    vel, _, pressure = primitives(mine)
    mine_flux = fluxes(mine, vel[0], pressure, 0)
    for v in range(VARS):
        du, df = near[v] - mine[v], near_flux[v] - mine_flux[v]
        far = -0.0625 * jnp.where(j < 2, pltpu.roll(du, CX - 2, 1), pltpu.roll(du, 2, 1))
        right = pltpu.roll(-0.5 * df + 0.25 * du, CX - 1, 1)
        left = pltpu.roll(0.5 * df + 0.25 * du, 1, 1)
        XC[v] = far + jnp.where(j == 1, right, 0.0) + jnp.where(j == 2, left, 0.0)

    row8 = iota((8, 4 * CX), 0)
    groups = ((0, 1), (2, 3), (4,))
    sums = []
    for t, group in enumerate(groups):

        for z in (0, 1, CZ - 2, CZ - 1):
            residual_plane(group, z)
        for v in group:
            for k, y in ((1, 0), (0, 1), (2, CY - 2), (3, CY - 1)):
                for c in range(CZ // 8):
                    lines = pl.ds(8 * c * PLANE + y, 8, stride=PLANE)
                    F[v, lines, :] = F[v, lines, :] + HY[k, v, 8 * c : 8 * c + 8, :]

        def second_pass(step, sums, group=group):
            sums = list(sums)
            for k in range(4):
                z = 4 * step + k
                here = pl.ds(pl.multiple_of(z * PLANE, PLANE), PLANE)
                for i, v in enumerate(group):
                    fix = pltpu.roll(XC[v], (2 * CX - 2 - 4 * z) & (CX - 1), 1)
                    r = F[v, here, :] + jnp.where(ends, fix, 0.0)
                    sums[i] = sums[i] + r * r
                    FS[v, here, 0:CX], FS[v, here, CX : 2 * CX] = split(r)
            return sums

        sums += lax.fori_loop(0, CZ // 4, second_pass, [jnp.zeros((CY, CX), F32)] * len(group))
        pair = [jnp.zeros((8, ROWS), F32)] * 2
        for v in group:
            tile = jnp.where(iota((8, CX), 0) < 2, inv_x[v, 0:8, :], pltpu.roll(inv_x[v, CX - 8 : CX, :], 4, 0))
            if v & 1:
                tile = pltpu.roll(tile, 4, 0)
            hi, lo = split(tile)
            left = jnp.concatenate([jnp.concatenate([hi, hi], 1), jnp.concatenate([lo, lo], 1)], 0)
            both = dot_nt(left, FS[v])
            pair[v & 1] = both[0:8] + both[8:16]
        XR[t, ix] = jnp.where(row8 < 4, pair[0], pair[1])
        for d in range(1, px):
            remote(XR.at[t, ix], XR.at[t, ix], xs, xrv.at[t], peer("gx", d)).start()

    stat_row = iota((8, CX), 0)
    tile = jnp.where(stat_row == VARS, jnp.max(top), 0.0)
    for v in range(VARS):
        tile = jnp.where(stat_row == v, jnp.sum(sums[v]), tile)
    STX[ix] = tile
    for d in range(1, px):
        remote(STX.at[ix], STX.at[ix], ss.at[0], sr.at[0], peer("gx", d)).start()

    def combine(ref, n):
        total = ref[0]
        for k in range(1, n):
            total = jnp.where(stat_row == VARS, jnp.maximum(total, ref[k]), total + ref[k])
        return total

    def local_x(v, carry):
        XL[v] = nt2(FS[v], AX[v])
        return carry

    lax.fori_loop(0, VARS, local_x, 0, unroll=True)

    def exchange(axis, me, n, rows, src, dst, v, send, recv):
        mine = pl.ds(pl.multiple_of(me * rows, rows), rows)
        for d in range(1, n):
            to = peer(axis, d)
            there = pl.ds(pl.multiple_of(to[axis] * rows, rows), rows)
            remote(src.at[v, there], dst.at[v, mine], send, recv, to).start()
        dst[v, mine, :] = src[v, mine, :]

    faces = ((0, 0), (0, 1), (1, 6), (1, 7))

    def local_yz(group):
        for v in group:
            for half in range(2):
                here = slice(256 * half, 256 * half + 256)
                field = XL[v, here, :] - nt2(CT[v >> 1, here, :], WX[v])
                for g in range(2):
                    solved = mm2(MY[v], field[128 * g : 128 * g + 128])
                    for k in range(16):
                        z, h = 8 * (2 * half + g) + k // 2, k & 1
                        FG[v & 1, h, 8 * z : 8 * z + 8, :] = solved[8 * k : 8 * k + 8]
        for v in group:
            for h in range(2):
                G[v, h] = mm2(MZ[v], FG[v & 1, h])
        for v in group:
            for h in range(2):
                for k, z in enumerate((0, 1, CZ - 2, CZ - 1)):
                    ZF[v, pl.ds(yc * k + h, 8, stride=zr), :] = G[v, h, 8 * z : 8 * z + 8, :]
            exchange("gz", iz, pz, zr, ZF, ZR1, v, zsem, zr1s.at[v])
            for k, (h, y) in enumerate(faces):
                for t in range(zc):
                    YF[v, pl.ds(zc * k + t, 8, stride=yr), :] = G[v, h, pl.ds(64 * t + y, 8, stride=8), :]
            exchange("gy", iy, py, yr, YF, YR1, v, ysem, yr1s.at[v])

    for t, group in enumerate(groups):
        drain(XR.at[t, pl.ds(0, px - 1)], xrv.at[t])
        factors = mm3(*split(LX[t]), XR[t].reshape(8 * px, ROWS))
        factors = jnp.concatenate([factors, jnp.zeros((CX - 8, ROWS), F32)], axis=0).T
        CT[t] = jnp.concatenate(split(factors), axis=1)
        local_yz(group)
        if t == 0:
            drain(STX.at[pl.ds(0, px - 1)], sr.at[0])
            STY[iy] = combine(STX, px)
            for d in range(1, py):
                remote(STY.at[iy], STY.at[iy], ss.at[1], sr.at[1], peer("gy", d)).start()
        if t == 2:
            drain(STY.at[pl.ds(0, py - 1)], sr.at[1])
            STZ[iz] = combine(STY, py)
            for d in range(1, pz):
                remote(STZ.at[iz], STZ.at[iz], ss.at[2], sr.at[2], peer("gz", d)).start()

    def build_reduced(v, carry):
        def reduced(red, n, speed):
            g = coupling((4 * n, 4 * n), speed, lambda r: ((r >> 2) << 2, r & 3))
            return split(exact_dot(g, red))

        y_side = lambda r: (r >> log2(zc), r & (zc - 1))
        hi, lo = expand(reduced(red_y[v], py, adv[1, v]), 4 * CZ, y_side, 4 * CZ, y_side)
        KY[v, 0:CX, :], KY[v, CX : 2 * CX, :] = hi, lo
        z_side = lambda r: (r >> log2(yc), r & (yc - 1))
        KZ[0, v], KZ[1, v] = expand(reduced(red_z[v], pz, adv[2, v]), 4 * CY, z_side, 4 * CY, z_side)
        return carry

    lax.fori_loop(0, VARS, build_reduced, 0, unroll=True)

    def reduced_lines(v, carry):
        drain(YR1.at[v, pl.ds(0, (py - 1) * yr)], yr1s.at[v])
        Y2[v] = mm2(KY[v], YR1[v])
        exchange("gy", iy, py, yr, Y2, YR2, v, y2sem, yr2s.at[v])
        drain(ZR1.at[v, pl.ds(0, (pz - 1) * zr)], zr1s.at[v])
        Z2[v] = mm3(KZ[0, v], KZ[1, v], ZR1[v])
        exchange("gz", iz, pz, zr, Z2, ZR2, v, z2sem, zr2s.at[v])
        return carry

    lax.fori_loop(0, VARS, reduced_lines, 0)

    def build_columns(v, carry):
        SY[v] = columns(inv_y[v], CY)
        SZ[v] = columns(inv_z[v], CZ)
        return carry

    lax.fori_loop(0, VARS, build_columns, 0, unroll=True)

    def correct_z(v, carry):
        drain(ZR2.at[v, pl.ds(0, (pz - 1) * zr)], zr2s.at[v])
        for k, (h, y) in enumerate(faces):
            E[v, 4 * k : 4 * k + 4, :] = ZR2[v, pl.ds(zr * y + h, 4, stride=yc), :]
        mine = pl.ds(pl.multiple_of(16 * iy, 16), 16)
        for d in range(1, py):
            remote(E.at[v], ER.at[v, mine], es, ers.at[v], peer("gy", d)).start()
        ER[v, mine, :] = E[v]
        factor = [[ZR2[v, pl.ds(yc * k + h, 8, stride=zr), :] for h in range(2)] for k in range(4)]
        for z in range(CZ):
            weight = [jnp.broadcast_to(SZ[v, z : z + 1, CX * k : CX * k + CX], (8, CX)) for k in range(4)]
            for h in range(2):
                total = G[v, h, 8 * z : 8 * z + 8, :]
                for k in range(4):
                    total = total - weight[k] * factor[k][h]
                G[v, h, 8 * z : 8 * z + 8, :] = total
        return carry

    lax.fori_loop(0, VARS, correct_z, 0)
    drain(STZ.at[pl.ds(0, pz - 1)], sr.at[2])
    stats = combine(STZ, pz)
    step = 8000.0 / stats[VARS : VARS + 1]
    rms[...] = jnp.sqrt(stats / float(px * py * pz * ROWS * CX))

    def finish(v, carry):
        drain(YR2.at[v, pl.ds(0, (py - 1) * yr)], yr2s.at[v])
        drain(ER.at[v, pl.ds(0, (py - 1) * 16)], ers.at[v])
        left = [KY[v, pl.ds(pl.multiple_of(part * CX + 16 * iy, 16), 16), :] for part in range(2)]
        cross = mm2(jnp.concatenate(left, axis=0), ER[v])
        for t in range(zc):
            weight = [SZ[v, 8 * t : 8 * t + 8, CX * j : CX * j + CX] for j in range(4)]
            for k in range(4):
                total = YR2[v, pl.ds(zc * k + t, 8, stride=yr), :]
                for j in range(4):
                    total = total - weight[j] * jnp.broadcast_to(cross[4 * k + j : 4 * k + j + 1], (8, CX))
                CF[k, 8 * t : 8 * t + 8, :] = total
        column = [SY[v, :, CX * k : CX * k + CX] * step for k in range(4)]
        for z in range(CZ):
            line = [jnp.broadcast_to(CF[k, z : z + 1, :], (8, CX)) for k in range(4)]
            for h in range(2):
                total = step * G[v, h, 8 * z : 8 * z + 8, :]
                for k in range(4):
                    total = total - column[k][8 * h : 8 * h + 8] * line[k]
                F[v, z * PLANE + 8 * h : z * PLANE + 8 * h + 8, :] = total
        return carry

    lax.fori_loop(0, VARS, finish, 0)
    for copy in halos:
        copy.wait_send()
    drain(XR.at[:, pl.ds(0, px - 1)], xs)
    drain(STX.at[pl.ds(0, px - 1)], ss.at[0])
    drain(STY.at[pl.ds(0, py - 1)], ss.at[1])
    drain(STZ.at[pl.ds(0, pz - 1)], ss.at[2])
    drain(YF.at[:, pl.ds(0, (py - 1) * yr)], ysem)
    drain(Y2.at[:, pl.ds(0, (py - 1) * yr)], y2sem)
    drain(ZF.at[:, pl.ds(0, (pz - 1) * zr)], zsem)
    drain(Z2.at[:, pl.ds(0, (pz - 1) * zr)], z2sem)
    drain(ER.at[:, pl.ds(0, (py - 1) * 16)], es)


def shards(px, py, pz, flow_state, advection, *tables):
    vmem = pl.BlockSpec(memory_space=pltpu.VMEM)
    hbm = pl.BlockSpec(memory_space=pltpu.HBM)
    f32 = lambda *shape: pltpu.VMEM(shape, F32)
    b16 = lambda *shape: pltpu.VMEM(shape, BF16)
    dma = pltpu.SemaphoreType.DMA
    field = (VARS, ROWS, CX)
    padded_rows = ROWS + 4 * PLANE
    y_face, z_face = (VARS, 4 * CZ, CX), (VARS, 4 * CY, CX)
    update, rms = pl.pallas_call(
        functools.partial(kernel, px, py, pz),
        out_shape=(jax.ShapeDtypeStruct(field, F32), jax.ShapeDtypeStruct((8, CX), F32)),
        in_specs=[hbm] * 8,
        out_specs=(vmem, vmem),
        scratch_shapes=[
            pltpu.SMEM(advection.shape, F32), *[f32(*table.shape) for table in tables],
            f32(VARS, padded_rows, CX), f32(3, padded_rows, CX), f32(4, padded_rows, CX),
            f32(2, VARS, 2 * CZ, CX), f32(2, VARS, 2 * CZ, CX), f32(4, VARS, CZ, CX),
            f32(VARS, CY, CX), f32(2, VARS, CY, CX), f32(VARS, CY, CX),
            b16(VARS, ROWS, 2 * CX), f32(*field), f32(VARS, 2, ROWS // 2, CX), f32(2, 2, ROWS // 2, CX),
            f32(3, px, 8, ROWS), b16(3, ROWS, 2 * CX),
            *[f32(*y_face)] * 4, *[f32(*z_face)] * 4,
            f32(VARS, 16, CX), f32(VARS, 16 * py, CX), f32(4, CZ, CX),
            f32(px, 8, CX), f32(py, 8, CX), f32(pz, 8, CX),
            b16(VARS, 2 * CX, 2 * CX), b16(VARS, 2 * CX, 2 * CX), f32(3, 8, 8 * px),
            b16(VARS, 2 * CX, CX), b16(VARS, 512, 256),
            b16(VARS, 8 * CZ, 4 * CZ), b16(2, VARS, 4 * CY, 4 * CY),
            f32(VARS, CY, 4 * CX), f32(VARS, CZ, 4 * CX),
            dma((8,)), dma((6,)), dma((6,)), dma, dma((3,)),
            *[dma, dma((VARS,))] * 5,
            dma((3,)), dma((3,)),
        ],
        compiler_params=pltpu.CompilerParams(
            collective_id=0, has_side_effects=True, vmem_limit_bytes=32 * 1024 * 1024
        ),
        name="adi_step",
    )(*[pltpu.with_memory_space_constraint(x, pltpu.HBM) for x in (advection, flow_state.reshape(field), *tables)])
    return update.reshape(flow_state.shape), rms[:VARS, 0]


def solution(mesh):
    sizes = [mesh.shape[axis] for axis in ("gx", "gy", "gz")]
    return jax.shard_map(
        functools.partial(shards, *sizes),
        mesh=mesh,
        in_specs=(P(None, "gz", "gy", "gx"), P(), P(), P(), P(), P(), P(), P()),
        out_specs=(P(None, "gz", "gy", "gx"), P()),
        check_vma=False,
    )
```

time: 47.4 us -> 42.8 us (0.903)
  Pallas kernels: 45 us -> 40.4 us
    pallas_call x1, Pallas kernels: 45 us -> 40.4 us  [shards(): pl.pallas_call(functools.partial(kernel, px, py, pz), out_shape=(jax.Shap...]
where the time goes in v3:
time: 42.8 us; the launch traced here: 42.7 us
  Pallas kernels  40.4 us (94%)
  local copies, waits for them, and re-layouts  1.68 us (4%)
  between operations  0.64 us (1%)
    pallas_call x1, Pallas kernels, shards(): pl.pallas_call(functools.partial(kernel, px, py, pz), out_shape=(jax.Shap...  40.4 us
    unnamed x1, local copies, waits for them, and re-layouts  1.06 us

profile of v3, /device:TPU:1, one launch (start us, length us, event | category | flops | bytes accessed | tf_op | source)
XLA Modules:
  0.0 42.7 jit_solution(1021757169442814633)
XLA Ops:
  0.6 40.4 %adi_step.1 = (f32[5,512,128]{2,1,0:T(8,128)S(1)}, f32[8,128]{1,0:T(8,128)S(1)}) custom-call(f32[3,5]{1,0:T(4,128)} %tab_adv.1, f32[5,512,128]{2,1,0:T(8,128)} %bitcast.3, f32[5,128,128]{2,1,0:T(8,128)} %refs_0_.1, f32[5,16,16]{2,1,0:T(8,128)} %refs_1_.1, f32[5,32,32]{2,1,0:T(8,128)} %refs_2_.1, f32[5,16,16]{2,1,0:T(8,128)} %refs_3_.1, ...), custom_call_target="tpu_custom_call" | custom-call | tf_op jit(solution)/shard_map/adi_step/pallas_call | solution.py:546
  41.0 0.6 %slice_reduce_fusion = f32[5]{0:T(128)} fusion(f32[8,128]{1,0:T(8,128)S(1)} %get-tuple-element.5), kind=kLoop, calls=%fused_computation | loop fusion | bytes 40 | tf_op jit(solution)/shard_map/slice | solution.py:574
  41.6 1.1 %copy.11 = f32[5,32,16,128]{3,2,1,0:T(8,128)} copy(f32[5,32,16,128]{3,2,1,0:T(8,128)S(1)} %bitcast.2) | data formatting | bytes 2621440

commit v4 on v3

--- a/solution.py
+++ b/solution.py
@@ -59,33 +59,6 @@
 
 def edge(k, length):
     return jnp.where(k < 2, k, k + (length - 4))
-
-
-def expand(parts, rows, row_map, cols, col_map):
-    n, m = parts[0].shape
-    row_i, _ = row_map(iota((rows, n), 0))
-    pick_rows = one_hot(row_i == iota((rows, n), 1))
-    col_j, _ = col_map(iota((m, cols), 1))
-    pick_cols = one_hot(col_j == iota((m, cols), 0))
-    _, row_r = row_map(iota((rows, cols), 0))
-    _, col_c = col_map(iota((rows, cols), 1))
-    keep = row_r == col_c
-    return [
-        jnp.where(keep, dot(pick_rows, dot(part, pick_cols).astype(BF16)), 0.0).astype(BF16)
-        for part in parts
-    ]
-
-
-def coupling(shape, speed, row_of):
-    row, col = iota(shape, 0), iota(shape, 1)
-    base, k = row_of(row)
-    lower, upper = -0.5 * speed - 2.0, 0.5 * speed - 2.0
-    out = jnp.where((k == 0) & (col == base - 2), 0.5, 0.0)
-    out = out + jnp.where((k == 0) & (col == base - 1), lower, 0.0)
-    out = out + jnp.where((k == 1) & (col == base - 1), 0.5, 0.0)
-    out = out + jnp.where((k == 2) & (col == base + 4), 0.5, 0.0)
-    out = out + jnp.where((k == 3) & (col == base + 4), upper, 0.0)
-    return out + jnp.where((k == 3) & (col == base + 5), 0.5, 0.0)
 
 
 def primitives(u):
@@ -111,7 +84,7 @@
     (
         tab_x, tab_y, tab_z, tab_rx, tab_ry, tab_rz,
         F, rms,
-        adv, inv_x, inv_y, inv_z, red_x, red_y, red_z,
+        adv, inv_x, inv_y, inv_z, RX, RP,
         U, PR, FZ, YS, YH, HY, PK, XH, XC, FS, XL, G, FG, XR, CT,
         YF, YR1, Y2, YR2, ZF, ZR1, Z2, ZR2, E, ER, CF, STX, STY, STZ,
         AX, WX, LX, MY, MZ, KY, KZ, SY, SZ,
@@ -140,11 +113,16 @@
         pltpu.make_async_copy(src, dst, in_sem.at[1 + k])
         for k, (src, dst) in enumerate(zip(
             (tab_adv, tab_x, tab_y, tab_z, tab_rx, tab_ry, tab_rz),
-            (adv, inv_x, inv_y, inv_z, red_x, red_y, red_z),
+            (adv, inv_x, inv_y, inv_z, RX.at[:, pl.ds(8, 4 * px)], RP.at[0, :, pl.ds(8, 4 * py)], RP.at[1, :, pl.ds(8, 4 * pz)]),
         ))
     ]
     for copy in tables:
         copy.start()
+    for axis, n in enumerate((py, pz)):
+        for start in (0, 8 + 4 * n):
+            RP[axis, :, start : start + 8, :] = jnp.zeros((VARS, 8, 4 * n), F32)
+    for start in (0, 8 + 4 * px):
+        RX[:, start : start + 8, :] = jnp.zeros((VARS, 8, 4 * px), F32)
     barrier = pltpu.get_barrier_semaphore()
     for axis, n in (("gz", pz), ("gy", py), ("gx", px)):
         for d in range(1, n):
@@ -197,21 +175,14 @@
             FZ[k, here, :] = f
         return vel, internal
 
-    def first_pass(step, top):
-        for k in range(2):
-            base = pl.multiple_of(2 * PLANE + (2 * step + k) * PLANE, PLANE)
-            vel, internal = plane_primitives(base)
-            speed = jnp.abs(vel[0]) + jnp.abs(vel[1]) + jnp.abs(vel[2]) + jnp.sqrt(3.0 * 1.4 * 0.4 * internal)
-            top = jnp.maximum(top, speed)
-        return top
-
-    top = lax.fori_loop(0, CZ // 2, first_pass, jnp.zeros((CY, CX), F32))
+    top = jnp.zeros((CY, CX), F32)
+    for z in range(CZ):
+        vel, internal = plane_primitives((2 + z) * PLANE)
+        speed = jnp.abs(vel[0]) + jnp.abs(vel[1]) + jnp.abs(vel[2]) + jnp.sqrt(3.0 * 1.4 * 0.4 * internal)
+        top = jnp.maximum(top, speed)
 
     for copy in tables:
         copy.wait()
-    def exact_dot(a, b):
-        return mm3(*split(a), b)
-
     def columns(table, length):
         shape = (length, 4 * CX)
         pick = one_hot(iota(shape, 0) == edge(iota(shape, 1) >> 7, length))
@@ -235,19 +206,6 @@
         return carry
 
     lax.fori_loop(0, VARS, build_first, 0, unroll=True)
-    for t in range(3):
-        acc = jnp.zeros((8, 8 * px), F32)
-        for v in (2 * t, 2 * t + 1):
-            if v == VARS:
-                continue
-            own = coupling((8, 4 * px), adv[0, v], lambda r: (4 * ix, r & 3))
-            rows = exact_dot(own, red_x[v])
-            r, c = iota((4 * px, 8 * px), 0), iota((4 * px, 8 * px), 1)
-            wide = exact_dot(rows, jnp.where(r == ((c >> 3) << 2) + (c & 3), 1.0, 0.0))
-            r, c = iota((8, 8 * px), 0), iota((8, 8 * px), 1)
-            acc = acc + jnp.where(((r >> 2) == v - 2 * t) & (((c >> 2) & 1) == v - 2 * t), wide, 0.0)
-        LX[t] = acc
-
     ends = ((lane + 2) & (CX - 1)) < 4
 
     def residual_plane(group, z):
@@ -287,6 +245,7 @@
         return carry
 
     lax.fori_loop(0, (CZ - 4) // 2, interior, 0)
+
     def build_z(v, carry):
         wide = iota((CZ, 8 * CZ), 1)
         pick = one_hot(iota((CZ, 8 * CZ), 0) == (wide >> 3))
@@ -346,19 +305,14 @@
                     lines = pl.ds(8 * c * PLANE + y, 8, stride=PLANE)
                     F[v, lines, :] = F[v, lines, :] + HY[k, v, 8 * c : 8 * c + 8, :]
 
-        def second_pass(step, sums, group=group):
-            sums = list(sums)
-            for k in range(4):
-                z = 4 * step + k
-                here = pl.ds(pl.multiple_of(z * PLANE, PLANE), PLANE)
-                for i, v in enumerate(group):
-                    fix = pltpu.roll(XC[v], (2 * CX - 2 - 4 * z) & (CX - 1), 1)
-                    r = F[v, here, :] + jnp.where(ends, fix, 0.0)
-                    sums[i] = sums[i] + r * r
-                    FS[v, here, 0:CX], FS[v, here, CX : 2 * CX] = split(r)
-            return sums
-
-        sums += lax.fori_loop(0, CZ // 4, second_pass, [jnp.zeros((CY, CX), F32)] * len(group))
+        for v in group:
+            total = jnp.zeros((CY, CX), F32)
+            for z in range(CZ):
+                here = slice(z * PLANE, z * PLANE + PLANE)
+                r = F[v, here, :] + jnp.where(ends, pltpu.roll(XC[v], (2 * CX - 2 - 4 * z) % CX, 1), 0.0)
+                total = total + r * r
+                FS[v, here, 0:CX], FS[v, here, CX : 2 * CX] = split(r)
+            sums.append(total)
         pair = [jnp.zeros((8, ROWS), F32)] * 2
         for v in group:
             tile = jnp.where(iota((8, CX), 0) < 2, inv_x[v, 0:8, :], pltpu.roll(inv_x[v, CX - 8 : CX, :], 4, 0))
@@ -392,6 +346,50 @@
 
     lax.fori_loop(0, VARS, local_x, 0, unroll=True)
 
+    rows = []
+    for v in range(VARS):
+        near = [RX[v, pl.ds(8 + 4 * ix + at, 1), :] for at in (-2, -1, 4, 5)]
+        half = 0.5 * adv[0, v]
+        rows += [0.5 * near[0] + (-half - 2.0) * near[1], 0.5 * near[1],
+                 0.5 * near[2], (half - 2.0) * near[2] + 0.5 * near[3]]
+    rows = jnp.concatenate(rows + [jnp.zeros((4, 4 * px), F32)], axis=0)
+    r, c = iota((4 * px, 8 * px), 0), iota((4 * px, 8 * px), 1)
+    pick = one_hot(r == ((c >> 3) << 2) + (c & 3))
+    hi, lo = split(rows)
+    rows = dot(hi, pick) + dot(lo, pick)
+    own = ((iota((8, 8 * px), 1) >> 2) & 1) == (iota((8, 8 * px), 0) >> 2)
+    for t in range(3):
+        LX[t] = jnp.where(own, rows[8 * t : 8 * t + 8], 0.0)
+
+    def build_reduced(axis, n, lines, out):
+        shift = log2(lines)
+        cols = 4 * n * lines
+        pick = one_hot(iota((4 * n, cols), 0) == (iota((4 * n, cols), 1) >> shift))
+        pick = jnp.concatenate([pick, pick], axis=0)
+        spread = []
+        for v in range(VARS):
+            near = [RP[axis, v, pl.ds(8 + at, n, stride=4), :] for at in (-2, -1, 4, 5)]
+            half = 0.5 * adv[axis + 1, v]
+            rows = [0.5 * near[0] + (-half - 2.0) * near[1], 0.5 * near[1],
+                    0.5 * near[2], (half - 2.0) * near[2] + 0.5 * near[3]]
+            spread.append(dot(jnp.concatenate(split(jnp.concatenate(rows, axis=0)), axis=1), pick))
+        which = iota((n, cols), 1) & (lines - 1)
+        for v in range(VARS):
+            for k in range(4):
+                for line in range(lines):
+                    block = jnp.where(which == line, spread[v][n * k : n * k + n], 0.0)
+                    out[v, pl.ds(k * lines + line, n, stride=4 * lines), :] = block
+
+    build_reduced(0, py, zc, KY)
+    build_reduced(1, pz, yc, KZ)
+
+    def build_columns(v, carry):
+        SY[v] = columns(inv_y[v], CY)
+        SZ[v] = columns(inv_z[v], CZ)
+        return carry
+
+    lax.fori_loop(0, VARS, build_columns, 0, unroll=True)
+
     def exchange(axis, me, n, rows, src, dst, v, send, recv):
         mine = pl.ds(pl.multiple_of(me * rows, rows), rows)
         for d in range(1, n):
@@ -402,24 +400,24 @@
 
     faces = ((0, 0), (0, 1), (1, 6), (1, 7))
 
-    def local_yz(group):
-        for v in group:
-            for half in range(2):
-                here = slice(256 * half, 256 * half + 256)
-                field = XL[v, here, :] - nt2(CT[v >> 1, here, :], WX[v])
-                for g in range(2):
-                    solved = mm2(MY[v], field[128 * g : 128 * g + 128])
-                    for k in range(16):
-                        z, h = 8 * (2 * half + g) + k // 2, k & 1
-                        FG[v & 1, h, 8 * z : 8 * z + 8, :] = solved[8 * k : 8 * k + 8]
+    def local_y(group):
+        for v in group:
+            XL[v] = XL[v] - nt2(CT[v >> 1], WX[v])
+        for v in group:
+            for g in range(4):
+                solved = mm2(MY[v], XL[v, 128 * g : 128 * g + 128, :])
+                for k in range(16):
+                    z, h = 8 * g + k // 2, k & 1
+                    FG[v, h, 8 * z : 8 * z + 8, :] = solved[8 * k : 8 * k + 8]
         for v in group:
             for h in range(2):
-                G[v, h] = mm2(MZ[v], FG[v & 1, h])
+                G[v, h] = mm2(MZ[v], FG[v, h])
         for v in group:
             for h in range(2):
                 for k, z in enumerate((0, 1, CZ - 2, CZ - 1)):
                     ZF[v, pl.ds(yc * k + h, 8, stride=zr), :] = G[v, h, 8 * z : 8 * z + 8, :]
             exchange("gz", iz, pz, zr, ZF, ZR1, v, zsem, zr1s.at[v])
+        for v in group:
             for k, (h, y) in enumerate(faces):
                 for t in range(zc):
                     YF[v, pl.ds(zc * k + t, 8, stride=yr), :] = G[v, h, pl.ds(64 * t + y, 8, stride=8), :]
@@ -430,49 +428,39 @@
         factors = mm3(*split(LX[t]), XR[t].reshape(8 * px, ROWS))
         factors = jnp.concatenate([factors, jnp.zeros((CX - 8, ROWS), F32)], axis=0).T
         CT[t] = jnp.concatenate(split(factors), axis=1)
-        local_yz(group)
-        if t == 0:
+        local_y(group)
+        if t == 1:
             drain(STX.at[pl.ds(0, px - 1)], sr.at[0])
             STY[iy] = combine(STX, px)
             for d in range(1, py):
                 remote(STY.at[iy], STY.at[iy], ss.at[1], sr.at[1], peer("gy", d)).start()
-        if t == 2:
-            drain(STY.at[pl.ds(0, py - 1)], sr.at[1])
-            STZ[iz] = combine(STY, py)
-            for d in range(1, pz):
-                remote(STZ.at[iz], STZ.at[iz], ss.at[2], sr.at[2], peer("gz", d)).start()
-
-    def build_reduced(v, carry):
-        def reduced(red, n, speed):
-            g = coupling((4 * n, 4 * n), speed, lambda r: ((r >> 2) << 2, r & 3))
-            return split(exact_dot(g, red))
-
-        y_side = lambda r: (r >> log2(zc), r & (zc - 1))
-        hi, lo = expand(reduced(red_y[v], py, adv[1, v]), 4 * CZ, y_side, 4 * CZ, y_side)
-        KY[v, 0:CX, :], KY[v, CX : 2 * CX, :] = hi, lo
-        z_side = lambda r: (r >> log2(yc), r & (yc - 1))
-        KZ[0, v], KZ[1, v] = expand(reduced(red_z[v], pz, adv[2, v]), 4 * CY, z_side, 4 * CY, z_side)
-        return carry
-
-    lax.fori_loop(0, VARS, build_reduced, 0, unroll=True)
-
-    def reduced_lines(v, carry):
+    def both_parts(matrix):
+        return jnp.concatenate(split(matrix), axis=0)
+
+    def reduced_z(v):
+        drain(ZR1.at[v, pl.ds(0, (pz - 1) * zr)], zr1s.at[v])
+        Z2[v] = mm2(both_parts(KZ[v]), ZR1[v])
+        exchange("gz", iz, pz, zr, Z2, ZR2, v, z2sem, zr2s.at[v])
+
+    def reduced_y(v):
         drain(YR1.at[v, pl.ds(0, (py - 1) * yr)], yr1s.at[v])
-        Y2[v] = mm2(KY[v], YR1[v])
+        Y2[v] = mm2(both_parts(KY[v]), YR1[v])
         exchange("gy", iy, py, yr, Y2, YR2, v, y2sem, yr2s.at[v])
-        drain(ZR1.at[v, pl.ds(0, (pz - 1) * zr)], zr1s.at[v])
-        Z2[v] = mm3(KZ[0, v], KZ[1, v], ZR1[v])
-        exchange("gz", iz, pz, zr, Z2, ZR2, v, z2sem, zr2s.at[v])
-        return carry
-
-    lax.fori_loop(0, VARS, reduced_lines, 0)
-
-    def build_columns(v, carry):
-        SY[v] = columns(inv_y[v], CY)
-        SZ[v] = columns(inv_z[v], CZ)
-        return carry
-
-    lax.fori_loop(0, VARS, build_columns, 0, unroll=True)
+
+    reduced_y(0)
+    reduced_y(1)
+    reduced_z(0)
+    reduced_z(1)
+    drain(STY.at[pl.ds(0, py - 1)], sr.at[1])
+    STZ[iz] = combine(STY, py)
+    for d in range(1, pz):
+        remote(STZ.at[iz], STZ.at[iz], ss.at[2], sr.at[2], peer("gz", d)).start()
+    reduced_y(2)
+    reduced_y(3)
+    reduced_z(2)
+    reduced_z(3)
+    reduced_y(4)
+    reduced_z(4)
 
     def correct_z(v, carry):
         drain(ZR2.at[v, pl.ds(0, (pz - 1) * zr)], zr2s.at[v])
@@ -492,7 +480,7 @@
                 G[v, h, 8 * z : 8 * z + 8, :] = total
         return carry
 
-    lax.fori_loop(0, VARS, correct_z, 0)
+    lax.fori_loop(0, VARS, correct_z, 0, unroll=True)
     drain(STZ.at[pl.ds(0, pz - 1)], sr.at[2])
     stats = combine(STZ, pz)
     step = 8000.0 / stats[VARS : VARS + 1]
@@ -501,8 +489,7 @@
     def finish(v, carry):
         drain(YR2.at[v, pl.ds(0, (py - 1) * yr)], yr2s.at[v])
         drain(ER.at[v, pl.ds(0, (py - 1) * 16)], ers.at[v])
-        left = [KY[v, pl.ds(pl.multiple_of(part * CX + 16 * iy, 16), 16), :] for part in range(2)]
-        cross = mm2(jnp.concatenate(left, axis=0), ER[v])
+        cross = mm2(both_parts(KY[v, pl.ds(pl.multiple_of(16 * iy, 16), 16), :]), ER[v])
         for t in range(zc):
             weight = [SZ[v, 8 * t : 8 * t + 8, CX * j : CX * j + CX] for j in range(4)]
             for k in range(4):
@@ -520,7 +507,7 @@
                 F[v, z * PLANE + 8 * h : z * PLANE + 8 * h + 8, :] = total
         return carry
 
-    lax.fori_loop(0, VARS, finish, 0)
+    lax.fori_loop(0, VARS, finish, 0, unroll=True)
     for copy in halos:
         copy.wait_send()
     drain(XR.at[:, pl.ds(0, px - 1)], xs)
@@ -549,18 +536,19 @@
         in_specs=[hbm] * 8,
         out_specs=(vmem, vmem),
         scratch_shapes=[
-            pltpu.SMEM(advection.shape, F32), *[f32(*table.shape) for table in tables],
+            pltpu.SMEM(advection.shape, F32), *[f32(*table.shape) for table in tables[:3]], f32(VARS, 4 * px + 16, 4 * px),
+            f32(2, VARS, 4 * max(py, pz) + 16, 4 * max(py, pz)),
             f32(VARS, padded_rows, CX), f32(3, padded_rows, CX), f32(4, padded_rows, CX),
             f32(2, VARS, 2 * CZ, CX), f32(2, VARS, 2 * CZ, CX), f32(4, VARS, CZ, CX),
             f32(VARS, CY, CX), f32(2, VARS, CY, CX), f32(VARS, CY, CX),
-            b16(VARS, ROWS, 2 * CX), f32(*field), f32(VARS, 2, ROWS // 2, CX), f32(2, 2, ROWS // 2, CX),
+            b16(VARS, ROWS, 2 * CX), f32(*field), f32(VARS, 2, ROWS // 2, CX), f32(VARS, 2, ROWS // 2, CX),
             f32(3, px, 8, ROWS), b16(3, ROWS, 2 * CX),
             *[f32(*y_face)] * 4, *[f32(*z_face)] * 4,
             f32(VARS, 16, CX), f32(VARS, 16 * py, CX), f32(4, CZ, CX),
             f32(px, 8, CX), f32(py, 8, CX), f32(pz, 8, CX),
             b16(VARS, 2 * CX, 2 * CX), b16(VARS, 2 * CX, 2 * CX), f32(3, 8, 8 * px),
             b16(VARS, 2 * CX, CX), b16(VARS, 512, 256),
-            b16(VARS, 8 * CZ, 4 * CZ), b16(2, VARS, 4 * CY, 4 * CY),
+            f32(VARS, 4 * CZ, 4 * CZ), f32(VARS, 4 * CY, 4 * CY),
             f32(VARS, CY, 4 * CX), f32(VARS, CZ, 4 * CX),
             dma((8,)), dma((6,)), dma((6,)), dma, dma((3,)),
             *[dma, dma((VARS,))] * 5,

time: 42.8 us -> 39.9 us (0.932)
  Pallas kernels: 40.4 us -> 37.5 us
    pallas_call x1, Pallas kernels: 40.4 us -> 37.5 us  [shards(): pl.pallas_call(functools.partial(kernel, px, py, pz), out_shape=(jax.Shap...]
where the time goes in v4:
time: 39.9 us; the launch traced here: 39.8 us
  Pallas kernels  37.5 us (94%)
  local copies, waits for them, and re-layouts  1.68 us (4%)
  between operations  0.64 us (2%)
    pallas_call x1, Pallas kernels, shards(): pl.pallas_call(functools.partial(kernel, px, py, pz), out_shape=(jax.Shap...  37.5 us
    unnamed x1, local copies, waits for them, and re-layouts  1.06 us

profile of v4, /device:TPU:1, one launch (start us, length us, event | category | flops | bytes accessed | tf_op | source)
XLA Modules:
  0.0 39.8 jit_solution(16060334904883164608)
XLA Ops:
  0.6 37.5 %adi_step.1 = (f32[5,512,128]{2,1,0:T(8,128)S(1)}, f32[8,128]{1,0:T(8,128)S(1)}) custom-call(f32[3,5]{1,0:T(4,128)} %tab_adv.1, f32[5,512,128]{2,1,0:T(8,128)} %bitcast.3, f32[5,128,128]{2,1,0:T(8,128)} %refs_0_.1, f32[5,16,16]{2,1,0:T(8,128)} %refs_1_.1, f32[5,32,32]{2,1,0:T(8,128)} %refs_2_.1, f32[5,16,16]{2,1,0:T(8,128)} %refs_3_.1, ...), custom_call_target="tpu_custom_call" | custom-call | tf_op jit(solution)/shard_map/adi_step/pallas_call | solution.py:533
  38.1 0.6 %slice_reduce_fusion = f32[5]{0:T(128)} fusion(f32[8,128]{1,0:T(8,128)S(1)} %get-tuple-element.5), kind=kLoop, calls=%fused_computation | loop fusion | bytes 40 | tf_op jit(solution)/shard_map/slice | solution.py:562
  38.8 1.1 %copy.11 = f32[5,32,16,128]{3,2,1,0:T(8,128)} copy(f32[5,32,16,128]{3,2,1,0:T(8,128)S(1)} %bitcast.2) | data formatting | bytes 2621440

commit v5 on v4

--- a/solution.py
+++ b/solution.py
@@ -103,6 +103,9 @@
             src_ref=src, dst_ref=dst, send_sem=send, recv_sem=recv,
             device_id=device, device_id_type=MESH,
         )
+
+    def others(n):
+        return sorted(range(1, n), key=lambda d: -min(d, n - d))
 
     def drain(ref, sem):
         pltpu.make_async_copy(ref, ref, sem).wait()
@@ -323,7 +326,7 @@
             both = dot_nt(left, FS[v])
             pair[v & 1] = both[0:8] + both[8:16]
         XR[t, ix] = jnp.where(row8 < 4, pair[0], pair[1])
-        for d in range(1, px):
+        for d in others(px):
             remote(XR.at[t, ix], XR.at[t, ix], xs, xrv.at[t], peer("gx", d)).start()
 
     stat_row = iota((8, CX), 0)
@@ -331,7 +334,7 @@
     for v in range(VARS):
         tile = jnp.where(stat_row == v, jnp.sum(sums[v]), tile)
     STX[ix] = tile
-    for d in range(1, px):
+    for d in others(px):
         remote(STX.at[ix], STX.at[ix], ss.at[0], sr.at[0], peer("gx", d)).start()
 
     def combine(ref, n):
@@ -392,7 +395,7 @@
 
     def exchange(axis, me, n, rows, src, dst, v, send, recv):
         mine = pl.ds(pl.multiple_of(me * rows, rows), rows)
-        for d in range(1, n):
+        for d in others(n):
             to = peer(axis, d)
             there = pl.ds(pl.multiple_of(to[axis] * rows, rows), rows)
             remote(src.at[v, there], dst.at[v, mine], send, recv, to).start()
@@ -432,7 +435,7 @@
         if t == 1:
             drain(STX.at[pl.ds(0, px - 1)], sr.at[0])
             STY[iy] = combine(STX, px)
-            for d in range(1, py):
+            for d in others(py):
                 remote(STY.at[iy], STY.at[iy], ss.at[1], sr.at[1], peer("gy", d)).start()
     def both_parts(matrix):
         return jnp.concatenate(split(matrix), axis=0)
@@ -447,27 +450,20 @@
         Y2[v] = mm2(both_parts(KY[v]), YR1[v])
         exchange("gy", iy, py, yr, Y2, YR2, v, y2sem, yr2s.at[v])
 
-    reduced_y(0)
-    reduced_y(1)
-    reduced_z(0)
-    reduced_z(1)
+    for v in range(VARS):
+        reduced_z(v)
+        reduced_y(v)
     drain(STY.at[pl.ds(0, py - 1)], sr.at[1])
     STZ[iz] = combine(STY, py)
-    for d in range(1, pz):
+    for d in others(pz):
         remote(STZ.at[iz], STZ.at[iz], ss.at[2], sr.at[2], peer("gz", d)).start()
-    reduced_y(2)
-    reduced_y(3)
-    reduced_z(2)
-    reduced_z(3)
-    reduced_y(4)
-    reduced_z(4)
 
     def correct_z(v, carry):
         drain(ZR2.at[v, pl.ds(0, (pz - 1) * zr)], zr2s.at[v])
         for k, (h, y) in enumerate(faces):
             E[v, 4 * k : 4 * k + 4, :] = ZR2[v, pl.ds(zr * y + h, 4, stride=yc), :]
         mine = pl.ds(pl.multiple_of(16 * iy, 16), 16)
-        for d in range(1, py):
+        for d in others(py):
             remote(E.at[v], ER.at[v, mine], es, ers.at[v], peer("gy", d)).start()
         ER[v, mine, :] = E[v]
         factor = [[ZR2[v, pl.ds(yc * k + h, 8, stride=zr), :] for h in range(2)] for k in range(4)]

time: 39.9 us -> 39.1 us (0.980)
  Pallas kernels: 37.5 us -> 36.6 us
    pallas_call x1, Pallas kernels: 37.5 us -> 36.6 us  [shards(): pl.pallas_call(functools.partial(kernel, px, py, pz), out_shape=(jax.Shap...]
where the time goes in v5:
time: 39.1 us; the launch traced here: 39 us
  Pallas kernels  36.6 us (94%)
  local copies, waits for them, and re-layouts  1.68 us (4%)
  between operations  0.64 us (2%)
    pallas_call x1, Pallas kernels, shards(): pl.pallas_call(functools.partial(kernel, px, py, pz), out_shape=(jax.Shap...  36.6 us
    unnamed x1, local copies, waits for them, and re-layouts  1.06 us

profile of v5, /device:TPU:1, one launch (start us, length us, event | category | flops | bytes accessed | tf_op | source)
XLA Modules:
  0.0 39.0 jit_solution(2708519341836923435)
XLA Ops:
  0.6 36.6 %adi_step.1 = (f32[5,512,128]{2,1,0:T(8,128)S(1)}, f32[8,128]{1,0:T(8,128)S(1)}) custom-call(f32[3,5]{1,0:T(4,128)} %tab_adv.1, f32[5,512,128]{2,1,0:T(8,128)} %bitcast.3, f32[5,128,128]{2,1,0:T(8,128)} %refs_0_.1, f32[5,16,16]{2,1,0:T(8,128)} %refs_1_.1, f32[5,32,32]{2,1,0:T(8,128)} %refs_2_.1, f32[5,16,16]{2,1,0:T(8,128)} %refs_3_.1, ...), custom_call_target="tpu_custom_call" | custom-call | tf_op jit(solution)/shard_map/adi_step/pallas_call | solution.py:529
  37.3 0.6 %slice_reduce_fusion = f32[5]{0:T(128)} fusion(f32[8,128]{1,0:T(8,128)S(1)} %get-tuple-element.5), kind=kLoop, calls=%fused_computation | loop fusion | bytes 40 | tf_op jit(solution)/shard_map/slice | solution.py:558
  37.9 1.1 %copy.11 = f32[5,32,16,128]{3,2,1,0:T(8,128)} copy(f32[5,32,16,128]{3,2,1,0:T(8,128)S(1)} %bitcast.2) | data formatting | bytes 2621440

commit v6 on v5

--- a/solution.py
+++ b/solution.py
@@ -88,7 +88,7 @@
         U, PR, FZ, YS, YH, HY, PK, XH, XC, FS, XL, G, FG, XR, CT,
         YF, YR1, Y2, YR2, ZF, ZR1, Z2, ZR2, E, ER, CF, STX, STY, STZ,
         AX, WX, LX, MY, MZ, KY, KZ, SY, SZ,
-        in_sem, hs, hr, xs, xrv, ysem, yr1s, y2sem, yr2s, zsem, zr1s, z2sem, zr2s, es, ers, ss, sr,
+        in_sem, hs, hr, xs, xrv, ysem, yr1s, y2sem, yr2s, zsem, zr1s, z2sem, zr2s, es, ers, ss, sr, known,
     ) = refs
     ix, iy, iz = lax.axis_index("gx"), lax.axis_index("gy"), lax.axis_index("gz")
     zc, yc = CZ // py, CY // pz
@@ -127,9 +127,22 @@
     for start in (0, 8 + 4 * px):
         RX[:, start : start + 8, :] = jnp.zeros((VARS, 8, 4 * px), F32)
     barrier = pltpu.get_barrier_semaphore()
-    for axis, n in (("gz", pz), ("gy", py), ("gx", px)):
-        for d in range(1, n):
+    axes = (("gz", pz), ("gy", py), ("gx", px))
+    for axis, _ in axes:
+        for d in (1, -1):
             pl.semaphore_signal(barrier, inc=1, device_id=peer(axis, d), device_id_type=MESH)
+
+    def spread(turn):
+        for a, (axis, n) in enumerate(axes):
+            if turn < n // 2:
+                for d in (1, -1):
+                    pl.semaphore_signal(known.at[a, turn - 1], inc=1, device_id=peer(axis, d), device_id_type=MESH)
+
+    def heard(turn):
+        for a, (axis, n) in enumerate(axes):
+            if turn < n // 2:
+                pl.semaphore_wait(known.at[a, turn - 1], 2)
+
     load.wait()
 
     def pack_rows(v, carry):
@@ -154,7 +167,8 @@
 
     lax.fori_loop(0, VARS, pack_lanes, 0, unroll=True)
 
-    pl.semaphore_wait(barrier, px + py + pz - 3)
+    pl.semaphore_wait(barrier, 6)
+    spread(1)
     last = 2 * PLANE + ROWS
     halos = [
         remote(flow.at[:, pl.ds(ROWS - 2 * PLANE, 2 * PLANE)], U.at[:, pl.ds(0, 2 * PLANE)],
@@ -263,6 +277,8 @@
         return carry
 
     lax.fori_loop(0, VARS, build_z, 0, unroll=True)
+    heard(1)
+    spread(2)
     for copy in halos:
         copy.wait_recv()
     plane_primitives(PLANE)
@@ -329,6 +345,8 @@
         for d in others(px):
             remote(XR.at[t, ix], XR.at[t, ix], xs, xrv.at[t], peer("gx", d)).start()
 
+    heard(2)
+    spread(3)
     stat_row = iota((8, CX), 0)
     tile = jnp.where(stat_row == VARS, jnp.max(top), 0.0)
     for v in range(VARS):
@@ -426,6 +444,7 @@
                     YF[v, pl.ds(zc * k + t, 8, stride=yr), :] = G[v, h, pl.ds(64 * t + y, 8, stride=8), :]
             exchange("gy", iy, py, yr, YF, YR1, v, ysem, yr1s.at[v])
 
+    heard(3)
     for t, group in enumerate(groups):
         drain(XR.at[t, pl.ds(0, px - 1)], xrv.at[t])
         factors = mm3(*split(LX[t]), XR[t].reshape(8 * px, ROWS))
@@ -548,7 +567,7 @@
             f32(VARS, CY, 4 * CX), f32(VARS, CZ, 4 * CX),
             dma((8,)), dma((6,)), dma((6,)), dma, dma((3,)),
             *[dma, dma((VARS,))] * 5,
-            dma((3,)), dma((3,)),
+            dma((3,)), dma((3,)), pltpu.SemaphoreType.REGULAR((3, 3)),
         ],
         compiler_params=pltpu.CompilerParams(
             collective_id=0, has_side_effects=True, vmem_limit_bytes=32 * 1024 * 1024

time: 39.1 us -> 38.4 us (0.982)
  Pallas kernels: 36.6 us -> 35.9 us
    pallas_call x1, Pallas kernels: 36.6 us -> 35.9 us  [shards(): pl.pallas_call(functools.partial(kernel, px, py, pz), out_shape=(jax.Shap...]
where the time goes in v6:
time: 38.4 us; the launch traced here: 38.3 us
  Pallas kernels  35.9 us (93%)
  local copies, waits for them, and re-layouts  1.68 us (4%)
  between operations  0.64 us (2%)
    pallas_call x1, Pallas kernels, shards(): pl.pallas_call(functools.partial(kernel, px, py, pz), out_shape=(jax.Shap...  35.9 us
    unnamed x1, local copies, waits for them, and re-layouts  1.06 us

profile of v6, /device:TPU:1, one launch (start us, length us, event | category | flops | bytes accessed | tf_op | source)
XLA Modules:
  0.0 38.3 jit_solution(15583678213024423791)
XLA Ops:
  0.6 35.9 %adi_step.1 = (f32[5,512,128]{2,1,0:T(8,128)S(1)}, f32[8,128]{1,0:T(8,128)S(1)}) custom-call(f32[3,5]{1,0:T(4,128)} %tab_adv.1, f32[5,512,128]{2,1,0:T(8,128)} %bitcast.3, f32[5,128,128]{2,1,0:T(8,128)} %refs_0_.1, f32[5,16,16]{2,1,0:T(8,128)} %refs_1_.1, f32[5,32,32]{2,1,0:T(8,128)} %refs_2_.1, f32[5,16,16]{2,1,0:T(8,128)} %refs_3_.1, ...), custom_call_target="tpu_custom_call" | custom-call | tf_op jit(solution)/shard_map/adi_step/pallas_call | solution.py:548
  36.6 0.6 %slice_reduce_fusion = f32[5]{0:T(128)} fusion(f32[8,128]{1,0:T(8,128)S(1)} %get-tuple-element.5), kind=kLoop, calls=%fused_computation | loop fusion | bytes 40 | tf_op jit(solution)/shard_map/slice | solution.py:577
  37.2 1.1 %copy.11 = f32[5,32,16,128]{3,2,1,0:T(8,128)} copy(f32[5,32,16,128]{3,2,1,0:T(8,128)S(1)} %bitcast.2) | data formatting | bytes 2621440

commit v7 on v6

--- a/solution.py
+++ b/solution.py
@@ -157,16 +157,6 @@
     lane = iota((CY, CX), 1)
     row = iota((CY, CX), 0)
 
-    def pack_lanes(v, carry):
-        acc = jnp.zeros((CY, CX), F32)
-        for z in range(CZ):
-            plane = U[v, pl.ds((2 + z) * PLANE, PLANE), :]
-            acc = jnp.where((lane >> 2) == z, pltpu.roll(plane, (4 * z + 2) % CX, 1), acc)
-        PK[v] = acc
-        return carry
-
-    lax.fori_loop(0, VARS, pack_lanes, 0, unroll=True)
-
     pl.semaphore_wait(barrier, 6)
     spread(1)
     last = 2 * PLANE + ROWS
@@ -180,7 +170,18 @@
         remote(PK, XH.at[0], hs.at[4], hr.at[4], peer("gx", 1)),
         remote(PK, XH.at[1], hs.at[5], hr.at[5], peer("gx", -1)),
     ]
-    for copy in halos:
+    for copy in halos[:4]:
+        copy.start()
+    def pack_lanes(v, carry):
+        acc = jnp.zeros((CY, CX), F32)
+        for z in range(CZ):
+            plane = U[v, pl.ds((2 + z) * PLANE, PLANE), :]
+            acc = jnp.where((lane >> 2) == z, pltpu.roll(plane, (4 * z + 2) % CX, 1), acc)
+        PK[v] = acc
+        return carry
+
+    lax.fori_loop(0, VARS, pack_lanes, 0, unroll=True)
+    for copy in halos[4:]:
         copy.start()
 
     def plane_primitives(base):
@@ -430,6 +431,8 @@
                 for k in range(16):
                     z, h = 8 * g + k // 2, k & 1
                     FG[v, h, 8 * z : 8 * z + 8, :] = solved[8 * k : 8 * k + 8]
+
+    def local_z(group):
         for v in group:
             for h in range(2):
                 G[v, h] = mm2(MZ[v], FG[v, h])
@@ -444,13 +447,19 @@
                     YF[v, pl.ds(zc * k + t, 8, stride=yr), :] = G[v, h, pl.ds(64 * t + y, 8, stride=8), :]
             exchange("gy", iy, py, yr, YF, YR1, v, ysem, yr1s.at[v])
 
-    heard(3)
-    for t, group in enumerate(groups):
+    def line_factors(t):
         drain(XR.at[t, pl.ds(0, px - 1)], xrv.at[t])
         factors = mm3(*split(LX[t]), XR[t].reshape(8 * px, ROWS))
         factors = jnp.concatenate([factors, jnp.zeros((CX - 8, ROWS), F32)], axis=0).T
         CT[t] = jnp.concatenate(split(factors), axis=1)
+
+    heard(3)
+    line_factors(0)
+    for t, group in enumerate(groups):
         local_y(group)
+        if t < 2:
+            line_factors(t + 1)
+        local_z(group)
         if t == 1:
             drain(STX.at[pl.ds(0, px - 1)], sr.at[0])
             STY[iy] = combine(STX, px)

time: 38.4 us -> 38 us (0.990)
  no operation moved by 1% of the time
where the time goes in v7:
time: 38 us; the launch traced here: 37.9 us
  Pallas kernels  35.6 us (94%)
  local copies, waits for them, and re-layouts  1.68 us (4%)
  between operations  0.64 us (2%)
    pallas_call x1, Pallas kernels, shards(): pl.pallas_call(functools.partial(kernel, px, py, pz), out_shape=(jax.Shap...  35.6 us
    unnamed x1, local copies, waits for them, and re-layouts  1.06 us

profile of v7, /device:TPU:1, one launch (start us, length us, event | category | flops | bytes accessed | tf_op | source)
XLA Modules:
  0.0 37.9 jit_solution(12728410141264785668)
XLA Ops:
  0.6 35.6 %adi_step.1 = (f32[5,512,128]{2,1,0:T(8,128)S(1)}, f32[8,128]{1,0:T(8,128)S(1)}) custom-call(f32[3,5]{1,0:T(4,128)} %tab_adv.1, f32[5,512,128]{2,1,0:T(8,128)} %bitcast.3, f32[5,128,128]{2,1,0:T(8,128)} %refs_0_.1, f32[5,16,16]{2,1,0:T(8,128)} %refs_1_.1, f32[5,32,32]{2,1,0:T(8,128)} %refs_2_.1, f32[5,16,16]{2,1,0:T(8,128)} %refs_3_.1, ...), custom_call_target="tpu_custom_call" | custom-call | tf_op jit(solution)/shard_map/adi_step/pallas_call | solution.py:557
  36.3 0.6 %slice_reduce_fusion = f32[5]{0:T(128)} fusion(f32[8,128]{1,0:T(8,128)S(1)} %get-tuple-element.5), kind=kLoop, calls=%fused_computation | loop fusion | bytes 40 | tf_op jit(solution)/shard_map/slice | solution.py:586
  36.9 1.1 %copy.11 = f32[5,32,16,128]{3,2,1,0:T(8,128)} copy(f32[5,32,16,128]{3,2,1,0:T(8,128)S(1)} %bitcast.2) | data formatting | bytes 2621440
